TPU v7x, 32 devices: a whole 2x2x4 slice. The times are simulated.
32 devices in a mesh: dp: 16 (over z, y, core), mlp: 2 (over x).
Axes of the slice: x: 2, y: 2, z: 4, core: 2. Of those that a mesh axis runs over, the one named last changes fastest.
Arguments:
- block_input: bfloat16 [16, 2, 160, 1024], P('dp', 'mlp'), may hold values from -6 to 6
- span_offset: int32 [16, 2], replicated, may hold values from 0 to 15, as said below
- ln_gain: float32 [1024], replicated, may hold values from 0.5 to 1.5
- ln_bias: float32 [1024], replicated, may hold values from -3 to 3
- w_qkv: bfloat16 [1024, 3072], replicated, may hold values from -0.25 to 0.25
- b_qkv: float32 [3072], replicated, may hold values from -3 to 3
- w_out: bfloat16 [1024, 1024], replicated, may hold values from -1 to 1
- b_out: float32 [1024], replicated, may hold values from -3 to 3
- w_up: bfloat16 [1024, 4096], P(None, 'mlp'), may hold values from -0.1875 to 0.1875
- b_up: float32 [4096], P('mlp'), may hold values from -3 to 3
- w_down: bfloat16 [4096, 1024], P('mlp'), may hold values from -0.09375 to 0.09375
- b_down: float32 [1024], replicated, may hold values from -3 to 3
- cotangent: bfloat16 [16, 2, 160, 1024], P('dp', 'mlp'), may hold values from -6 to 6
Outputs:
- output: bfloat16 [16, 2, 160, 1024], P('dp', 'mlp')
- grad_input: float32 [16, 2, 160, 1024], P('dp', 'mlp')
- grad_ln_gain: float32 [1024], P('mlp')
- grad_ln_bias: float32 [1024], P('mlp')
- grad_w_qkv: float32 [1024, 3072], P(None, 'mlp')
- grad_b_qkv: float32 [3072], P('mlp')
- grad_w_out: float32 [1024, 1024], P(None, 'mlp')
- grad_b_out: float32 [1024], P('mlp')
- grad_w_up: float32 [1024, 4096], P(None, 'mlp')
- grad_b_up: float32 [4096], P('mlp')
- grad_w_down: float32 [4096, 1024], P('mlp')
- grad_b_down: float32 [1024], P('mlp')
Inputs may be any that keep to these rules, and one draw needn't show every extreme that they name: For every sequence s, span_offset[:, s] is a permutation of 0 to 15.
All inputs are finite; a program needn't handle non-finite values.
Results may differ from a plain program's by a relative error of at most 0.02.
Values may be sent and summed in bfloat16 or wider, within the bound.
A program may use at most 256 MiB of HBM per device.

v0:
```python
import math

import jax
import jax.numpy as jnp
from jax import lax
from jax.sharding import PartitionSpec as P

HEADS = 16
HEAD_DIM = 64
ROT = 16


EPSILON = 1e-05
ROPE_BASE = 10000.0
SQRT_HALF = 1.0 / math.sqrt(2.0)
INV_ROOT_TWO_PI = 1.0 / math.sqrt(2.0 * math.pi)


def rotate(values, positions, sign_factor):
    half_rot = ROT // 2
    frequency = ROPE_BASE ** (-(jnp.arange(half_rot, dtype=jnp.float32) * 2.0 / ROT))
    angles = positions.astype(jnp.float32)[:, None] * frequency[None, :]
    cosine = jnp.cos(angles)[:, None, :]
    sine_part = sign_factor * jnp.sin(angles)[:, None, :]
    first_half = values[..., :half_rot]
    second_half = values[..., half_rot:ROT]
    return jnp.concatenate(
        [
            first_half * cosine - second_half * sine_part,
            second_half * cosine + first_half * sine_part,
            values[..., ROT:],
        ],
        axis=-1,
    )


def gelu_exact(values):
    return 0.5 * values * (1.0 + lax.erf(values * SQRT_HALF))


def gelu_slope(values):
    return (
        0.5 * (1.0 + lax.erf(values * SQRT_HALF))
        + values * jnp.exp(-0.5 * values * values) * INV_ROOT_TWO_PI
    )


def piece_count(total_rows):
    count_blocks = max(1, total_rows // 1024)
    while total_rows % count_blocks:
        count_blocks += 1
    return count_blocks


def row_positions(offsets, count_rows, tok_count):
    index_all = jnp.arange(count_rows, dtype=jnp.int32)
    span_of = index_all // tok_count
    within = index_all - span_of * tok_count
    matches = span_of[:, None] == jnp.arange(offsets.shape[0], dtype=jnp.int32)[None, :]
    offset_of = jnp.sum(jnp.where(matches, offsets[None, :], 0), axis=1)
    return offset_of * tok_count + within


def contract_rows(left_mat, right_mat):
    return lax.dot_general(
        left_mat, right_mat, (((0,), (0,)), ((), ())), preferred_element_type=jnp.float32
    )


def contract_cols(left_mat, right_mat):
    return lax.dot_general(
        left_mat, right_mat, (((1,), (1,)), ((), ())), preferred_element_type=jnp.float32
    )


def local(
    block_input,
    span_offset,
    ln_gain,
    ln_bias,
    w_qkv,
    b_qkv,
    w_out,
    b_out,
    w_up,
    b_up,
    w_down,
    b_down,
    cotangent,
):
    tok_count = block_input.shape[2]
    model_width = block_input.shape[3]
    scale_dot = 1.0 / math.sqrt(HEAD_DIM)
    span_here = lax.axis_index("dp")
    seq_here = lax.axis_index("mlp")
    offsets = lax.dynamic_index_in_dim(span_offset, seq_here, axis=1, keepdims=False)
    offset_here = lax.dynamic_index_in_dim(offsets, span_here, axis=0, keepdims=False)
    positions = offset_here * tok_count + jnp.arange(tok_count, dtype=jnp.int32)
    row_data = block_input[0, 0].astype(jnp.float32)
    centre = jnp.mean(row_data, axis=-1, keepdims=True)
    centred = row_data - centre
    spread = jnp.mean(centred * centred, axis=-1, keepdims=True)
    inv_scale = lax.rsqrt(spread + EPSILON)
    unit_rows = centred * inv_scale
    normed = (unit_rows * ln_gain + ln_bias).astype(jnp.bfloat16)
    project = jnp.dot(normed, w_qkv, preferred_element_type=jnp.float32) + b_qkv
    queries = rotate(
        project[:, :model_width].reshape(tok_count, HEADS, HEAD_DIM), positions, 1.0
    ).astype(jnp.bfloat16)
    keys_here = rotate(
        project[:, model_width : 2 * model_width].reshape(tok_count, HEADS, HEAD_DIM),
        positions,
        1.0,
    ).astype(jnp.bfloat16)
    values_here = (
        project[:, 2 * model_width :].reshape(tok_count, HEADS, HEAD_DIM).astype(jnp.bfloat16)
    )
    keys_flat = keys_here.reshape(tok_count, model_width)
    values_flat = values_here.reshape(tok_count, model_width)
    start_state = (
        jnp.zeros((tok_count, HEADS, HEAD_DIM), jnp.float32),
        jnp.zeros((HEADS, tok_count), jnp.float32),
    )
    keys_piece = lax.all_gather(keys_flat, "dp", axis=0, tiled=True)
    values_piece = lax.all_gather(values_flat, "dp", axis=0, tiled=True)
    piece_rows = keys_piece.shape[0]
    blocks = piece_count(piece_rows)
    sub_rows = piece_rows // blocks
    key_pos = row_positions(offsets, piece_rows, tok_count)

    def attend_one_block(state_now, packed):
        keys_blk, values_blk, pos_blk = packed
        key_heads = keys_blk.reshape(sub_rows, HEADS, HEAD_DIM)
        value_heads = values_blk.reshape(sub_rows, HEADS, HEAD_DIM)
        scores = (
            jnp.einsum("qhd,khd->hqk", queries, key_heads, preferred_element_type=jnp.float32)
            * scale_dot
        )
        allowed = pos_blk[None, :] <= positions[:, None]
        weights_exp = jnp.where(allowed[None], jnp.exp(scores), 0.0)
        mixed_sum, totals = state_now
        mixed_sum = mixed_sum + jnp.einsum(
            "hqk,khd->qhd",
            weights_exp.astype(jnp.bfloat16),
            value_heads,
            preferred_element_type=jnp.float32,
        )
        return ((mixed_sum, totals + jnp.sum(weights_exp, axis=-1)), None)

    state_now, _unused = lax.scan(
        attend_one_block,
        start_state,
        (
            keys_piece.reshape(blocks, sub_rows, model_width),
            values_piece.reshape(blocks, sub_rows, model_width),
            key_pos.reshape(blocks, sub_rows),
        ),
    )
    mixed_sum, totals = state_now
    attended = mixed_sum / totals.T[:, :, None]
    attended_low = attended.reshape(tok_count, model_width).astype(jnp.bfloat16)
    attn_branch = jnp.dot(attended_low, w_out, preferred_element_type=jnp.float32) + b_out
    normed_all = lax.all_gather(normed, "mlp", axis=0, tiled=True)
    up_proj = jnp.dot(normed_all, w_up, preferred_element_type=jnp.float32) + b_up
    activated = gelu_exact(up_proj).astype(jnp.bfloat16)
    mlp_branch = (
        lax.psum_scatter(
            jnp.dot(activated, w_down, preferred_element_type=jnp.float32).astype(jnp.bfloat16),
            "mlp",
            scatter_dimension=0,
            tiled=True,
        ).astype(jnp.float32)
        + b_down
    )
    output = (row_data + attn_branch + mlp_branch).astype(jnp.bfloat16)
    grad_out = cotangent[0, 0]
    grad_w_out = contract_rows(attended_low, grad_out)
    grad_bias_out = jnp.sum(grad_out.astype(jnp.float32), axis=0)
    grad_all = lax.all_gather(grad_out, "mlp", axis=0, tiled=True)
    grad_w_down = contract_rows(activated, grad_all)
    grad_act = contract_cols(grad_all, w_down)
    grad_up = (grad_act * gelu_slope(up_proj)).astype(jnp.bfloat16)
    grad_w_up = contract_rows(normed_all, grad_up)
    grad_b_up = jnp.sum(grad_up.astype(jnp.float32), axis=0)
    grad_norm_mlp = lax.psum_scatter(
        contract_cols(grad_up, w_up).astype(jnp.bfloat16), "mlp", scatter_dimension=0, tiled=True
    ).astype(jnp.float32)
    grad_att = contract_cols(grad_out, w_out).reshape(tok_count, HEADS, HEAD_DIM)
    grad_mixed = (grad_att / totals.T[:, :, None]).astype(jnp.bfloat16)
    grad_totals = ((-jnp.sum(grad_att * attended, axis=-1)).T / totals).astype(jnp.bfloat16)
    grad_totals_wide = grad_totals.astype(jnp.float32)[:, :, None]
    zero_heads = jnp.zeros((tok_count, HEADS, HEAD_DIM), jnp.float32)
    grad_query_sum = zero_heads
    keys_piece = lax.all_gather(keys_flat, "dp", axis=0, tiled=True)
    values_piece = lax.all_gather(values_flat, "dp", axis=0, tiled=True)
    piece_rows = keys_piece.shape[0]
    blocks = piece_count(piece_rows)
    back_sub_rows = piece_rows // blocks
    key_pos = row_positions(offsets, piece_rows, tok_count)

    def back_one_block(running_sum, packed):
        keys_blk, values_blk, pos_blk = packed
        key_heads = keys_blk.reshape(back_sub_rows, HEADS, HEAD_DIM)
        value_heads = values_blk.reshape(back_sub_rows, HEADS, HEAD_DIM)
        scores = (
            jnp.einsum("qhd,khd->hqk", queries, key_heads, preferred_element_type=jnp.float32)
            * scale_dot
        )
        allowed = pos_blk[None, :] <= positions[:, None]
        weights_exp = jnp.where(allowed[None], jnp.exp(scores), 0.0)
        grad_exp = jnp.einsum(
            "qhd,khd->hqk", grad_mixed, value_heads, preferred_element_type=jnp.float32
        )
        grad_scores = (weights_exp * (grad_exp + grad_totals_wide)).astype(jnp.bfloat16)
        running_sum = running_sum + scale_dot * jnp.einsum(
            "hqk,khd->qhd", grad_scores, key_heads, preferred_element_type=jnp.float32
        )
        grad_key_blk = scale_dot * jnp.einsum(
            "hqk,qhd->khd", grad_scores, queries, preferred_element_type=jnp.float32
        )
        grad_value_blk = jnp.einsum(
            "hqk,qhd->khd",
            weights_exp.astype(jnp.bfloat16),
            grad_mixed,
            preferred_element_type=jnp.float32,
        )
        joined = jnp.concatenate(
            [
                grad_key_blk.reshape(back_sub_rows, model_width),
                grad_value_blk.reshape(back_sub_rows, model_width),
            ],
            axis=1,
        )
        return (running_sum, joined)

    grad_query_sum, stacked = lax.scan(
        back_one_block,
        grad_query_sum,
        (
            keys_piece.reshape(blocks, back_sub_rows, model_width),
            values_piece.reshape(blocks, back_sub_rows, model_width),
            key_pos.reshape(blocks, back_sub_rows),
        ),
    )
    grad_kv_sum = stacked.reshape(piece_rows, 2 * model_width)
    grad_kv = lax.psum_scatter(
        grad_kv_sum.astype(jnp.bfloat16), "dp", scatter_dimension=0, tiled=True
    ).astype(jnp.float32)
    grad_keys = grad_kv[:, :model_width].reshape(tok_count, HEADS, HEAD_DIM)
    grad_values = grad_kv[:, model_width:].reshape(tok_count, HEADS, HEAD_DIM)
    grad_query_pre = rotate(grad_query_sum, positions, -1.0).reshape(tok_count, model_width)
    grad_key_pre = rotate(grad_keys, positions, -1.0).reshape(tok_count, model_width)
    grad_project = jnp.concatenate(
        [grad_query_pre, grad_key_pre, grad_values.reshape(tok_count, model_width)], axis=1
    ).astype(jnp.bfloat16)
    grad_w_qkv = contract_rows(normed, grad_project)
    grad_b_qkv = jnp.sum(grad_project.astype(jnp.float32), axis=0)
    grad_normed = contract_cols(grad_project, w_qkv) + grad_norm_mlp
    grad_ln_gain = jnp.sum(grad_normed * unit_rows, axis=0)
    grad_ln_bias = jnp.sum(grad_normed, axis=0)
    grad_unit = grad_normed * ln_gain
    grad_rows = inv_scale * (
        grad_unit
        - jnp.mean(grad_unit, axis=-1, keepdims=True)
        - unit_rows * jnp.mean(grad_unit * unit_rows, axis=-1, keepdims=True)
    )
    grad_input = (grad_out.astype(jnp.float32) + grad_rows).reshape(1, 1, tok_count, model_width)
    part_qkv, part_out, part_bqkv, part_bias, part_gain, part_shift = (
        lax.psum_scatter(
            grad_w_qkv.astype(jnp.bfloat16), "mlp", scatter_dimension=1, tiled=True
        ).astype(jnp.float32),
        lax.psum_scatter(
            grad_w_out.astype(jnp.bfloat16), "mlp", scatter_dimension=1, tiled=True
        ).astype(jnp.float32),
        lax.psum_scatter(
            grad_b_qkv.astype(jnp.bfloat16), "mlp", scatter_dimension=0, tiled=True
        ).astype(jnp.float32),
        lax.psum_scatter(
            grad_bias_out.astype(jnp.bfloat16), "mlp", scatter_dimension=0, tiled=True
        ).astype(jnp.float32),
        lax.psum_scatter(
            grad_ln_gain.astype(jnp.bfloat16), "mlp", scatter_dimension=0, tiled=True
        ).astype(jnp.float32),
        lax.psum_scatter(
            grad_ln_bias.astype(jnp.bfloat16), "mlp", scatter_dimension=0, tiled=True
        ).astype(jnp.float32),
    )
    summed = (
        lax.psum(part_qkv.astype(jnp.bfloat16), "dp").astype(jnp.float32),
        lax.psum(part_out.astype(jnp.bfloat16), "dp").astype(jnp.float32),
        lax.psum(part_bqkv.astype(jnp.bfloat16), "dp").astype(jnp.float32),
        lax.psum(part_bias.astype(jnp.bfloat16), "dp").astype(jnp.float32),
        lax.psum(part_gain.astype(jnp.bfloat16), "dp").astype(jnp.float32),
        lax.psum(part_shift.astype(jnp.bfloat16), "dp").astype(jnp.float32),
        lax.psum(grad_w_up.astype(jnp.bfloat16), "dp").astype(jnp.float32),
        lax.psum(grad_b_up.astype(jnp.bfloat16), "dp").astype(jnp.float32),
        lax.psum(grad_w_down.astype(jnp.bfloat16), "dp").astype(jnp.float32),
    )
    return (
        output.reshape(1, 1, tok_count, model_width),
        grad_input,
        summed[4],
        summed[5],
        summed[0],
        summed[2],
        summed[1],
        summed[3],
        summed[6],
        summed[7],
        summed[8],
        summed[3],
    )


def solution(mesh):
    return jax.shard_map(
        local,
        mesh=mesh,
        in_specs=(
            P("dp", "mlp", None, None),
            P(),
            P(),
            P(),
            P(),
            P(),
            P(),
            P(),
            P(None, "mlp"),
            P("mlp"),
            P("mlp", None),
            P(),
            P("dp", "mlp", None, None),
        ),
        out_specs=(
            P("dp", "mlp", None, None),
            P("dp", "mlp", None, None),
            P("mlp"),
            P("mlp"),
            P(None, "mlp"),
            P("mlp"),
            P(None, "mlp"),
            P("mlp"),
            P(None, "mlp"),
            P("mlp"),
            P("mlp", None),
            P("mlp"),
        ),
        check_vma=False,
    )
```

profile of v0, /device:TPU:0, one launch (start us, length us, event | category | flops | bytes accessed | tf_op | source)
XLA Modules:
  0.0 848.4 jit_solution(7495591158141131622)
XLA Ops:
  38.0 52.4 %all-gather.6.cloned.1.call-done = bf16[2560,1024]{1,0:T(8,128)(2,1)} async-done(((bf16[160,1024]{1,0:T(8,128)(2,1)}), bf16[2560,1024]{1,0:T(8,128)(2,1)}) %all-gather.6.cloned.1.call-update) | async-done | bytes 5242896 | tf_op jit(solution)/shard_map/all_gather | solution.py:124
  90.4 7.9 copy.85
  98.3 49.4 %all-gather.4.cloned.1.call-done = bf16[2560,1024]{1,0:T(8,128)(2,1)} async-done(((bf16[160,1024]{1,0:T(8,128)(2,1)}), bf16[2560,1024]{1,0:T(8,128)(2,1)}) %all-gather.4.cloned.1.call-update) | async-done | bytes 5242896 | tf_op jit(solution)/shard_map/all_gather | solution.py:125
  147.7 7.9 copy.84
  155.5 40.2 %while.26 = (s32[]{:T(128)}, f32[160,16,64]{0,2,1:T(8,128)}, f32[16,160]{1,0:T(8,128)S(1)}, bf16[2,1280,1024]{1,2,0:T(8,128)(2,1)}, s32[2,1280]{1,0:T(2,128)S(1)...) while((s32[]{:T(128)}, f32[160,16,64]{0,2,1:T(8,128)}, ...), condition=%wide.region_5.6_spmd.clone, body=%wide.region_3.5_spmd.clone.sunk | while | flops 859056768 | bytes 44253560 | solution.py:150
  160.1 6.5 fusion.124
  166.7 8.9 %fusion.125 = f32[160,16,64]{0,2,1:T(8,128)} fusion(bf16[1280,16,64]{0,2,1:T(8,128)(2,1)} %bitcast.209, f32[16,1280,160]{1,2,0:T(8,128)} %get-tuple-element.480, pred[160,1280]{1,0:T(8,128)(4,1)S(1)} %broadcast_compare_fusion.4, f32[160,16,64]{0,2,1:T(8,128)} %get-tuple-element.505, pred[]{:T(512)S(6)} %compare.6), kind=kOutput, calls=%fused_computation.10.clone.1 | convolution fusion | flops 429588480 | bytes 17244160 | tf_op jit(solution)/shard_map/while/body/eval_jaxpr/hqk,khd->qhd/dot_general | solution.py:142
  180.1 6.5 fusion.124
  186.7 9.1 %fusion.125 = f32[160,16,64]{0,2,1:T(8,128)} fusion(bf16[1280,16,64]{0,2,1:T(8,128)(2,1)} %bitcast.209, f32[16,1280,160]{1,2,0:T(8,128)} %get-tuple-element.480, pred[160,1280]{1,0:T(8,128)(4,1)S(1)} %broadcast_compare_fusion.4, f32[160,16,64]{0,2,1:T(8,128)} %get-tuple-element.505, pred[]{:T(512)S(6)} %compare.6), kind=kOutput, calls=%fused_computation.10.clone.1 | convolution fusion | flops 429588480 | bytes 17244160 | tf_op jit(solution)/shard_map/while/body/eval_jaxpr/hqk,khd->qhd/dot_general | solution.py:142
  198.7 110.9 %while.27 = (s32[]{:T(128)}, f32[160,16,64]{0,2,1:T(8,128)}, bf16[2,1280,2048]{2,1,0:T(8,128)(2,1)}, bf16[2,1280,1024]{1,2,0:T(8,128)(2,1)}, s32[2,1280]{1,0:T(2...) while((s32[]{:T(128)}, f32[160,16,64]{0,2,1:T(8,128)}, ...), condition=%wide.region_9.10_spmd.clone, body=%wide.region_8.9_spmd.clone.sunk | while | flops 2137170048 | bytes 206425072 | solution.py:236
  203.3 6.6 fusion.136
  210.2 9.9 %fusion.137 = bf16[16,160,1280]{2,1,0:T(8,128)(2,1)S(1)} fusion(f32[16,1280,160]{1,2,0:T(8,128)} %fusion.136, bf16[1280,16,64]{0,2,1:T(8,128)(2,1)} %bitcast.211, bf16[160,16,64]{0,2,1:T(8,128)(2,1)} %get-tuple-element.555, f32[16,160]{1,0:T(8,128)S(1)} %bitcast.219, pred[160,1280]{1,0:T(8,128)(4,1)S(1)} %broadcast_compare_fusion.5), kind=kOutput, calls=%fused_computation.20.clone.1 | convolution fusion | flops 435814400 | bytes 22824960 | tf_op jit(solution)/shard_map/while/body/eval_jaxpr/qhd,khd->hqk/dot_general | solution.py:211
  233.6 8.0 copy.108
  247.2 6.9 fusion.138
  258.5 6.6 fusion.136
  265.3 9.9 %fusion.137 = bf16[16,160,1280]{2,1,0:T(8,128)(2,1)S(1)} fusion(f32[16,1280,160]{1,2,0:T(8,128)} %fusion.136, bf16[1280,16,64]{0,2,1:T(8,128)(2,1)} %bitcast.211, bf16[160,16,64]{0,2,1:T(8,128)(2,1)} %get-tuple-element.555, f32[16,160]{1,0:T(8,128)S(1)} %bitcast.219, pred[160,1280]{1,0:T(8,128)(4,1)S(1)} %broadcast_compare_fusion.5), kind=kOutput, calls=%fused_computation.20.clone.1 | convolution fusion | flops 435814400 | bytes 22824960 | tf_op jit(solution)/shard_map/while/body/eval_jaxpr/qhd,khd->hqk/dot_general | solution.py:211
  288.8 8.0 copy.108
  302.4 7.1 fusion.138
  326.9 100.9 %reduce-scatter.8.cloned.1.call-done = bf16[160,2048]{1,0:T(8,128)(2,1)} async-done(((bf16[2560,2048]{1,0:T(8,128)(2,1)}), bf16[160,2048]{1,0:T(8,128)(2,1)}) %reduce-scatter.8.cloned.1.call-update) | async-done | bytes 655376 | tf_op jit(solution)/shard_map/reduce_scatter | solution.py:246
  442.0 17.8 %all_gather.16 = bf16[320,1024]{1,0:T(8,128)(2,1)S(1)} all-gather(bf16[160,1024]{1,0:T(8,128)(2,1)S(1)} %copy-done.8), channel_id=1, replica_groups=mesh['dp'=16,'mlp'=2] {'mlp'}, dimensions={0}, use_global_device_ids=true | all-gather | bytes 983040 | tf_op jit(solution)/shard_map/all_gather | solution.py:163
  459.9 5.7 multiply_convert_fusion
  469.2 9.4 %all-gather = bf16[1,1,320,1024]{3,2,1,0:T(8,128)(2,1)S(1)} all-gather(bf16[1,1,160,1024]{3,2,1,0:T(8,128)(2,1)S(1)} %copy-done.11), channel_id=2, replica_groups=mesh['dp'=16,'mlp'=2] {'mlp'}, dimensions={2}, use_global_device_ids=true | all-gather | bytes 983040 | tf_op jit(solution)/shard_map/all_gather | solution.py:179
  478.6 6.4 fusion.68
  488.6 6.1 convolution_convert_fusion.2
  499.1 49.9 %reduce-scatter.12.cloned.1.call-done = bf16[1024,1536]{1,0:T(8,128)(2,1)} async-done(((bf16[1024,3072]{1,0:T(8,128)(2,1)}), bf16[1024,1536]{1,0:T(8,128)(2,1)}) %reduce-scatter.12.cloned.1.call-update) | async-done | bytes 3145744 | tf_op jit(solution)/shard_map/reduce_scatter | solution.py:269
  551.5 16.2 %reduce-scatter.6.cloned.1.call-done = bf16[160,1024]{1,0:T(8,128)(2,1)} async-done(((bf16[320,1024]{1,0:T(8,128)(2,1)}), bf16[160,1024]{1,0:T(8,128)(2,1)}) %reduce-scatter.6.cloned.1.call-update) | async-done | bytes 327696 | tf_op jit(solution)/shard_map/reduce_scatter | solution.py:167
  570.4 15.7 %reduce-scatter.10.cloned.1.call-done = bf16[160,1024]{1,0:T(8,128)(2,1)} async-done(((bf16[320,1024]{1,0:T(8,128)(2,1)}), bf16[160,1024]{1,0:T(8,128)(2,1)}) %reduce-scatter.10.cloned.1.call-update) | async-done | bytes 327696 | tf_op jit(solution)/shard_map/reduce_scatter | solution.py:185
  586.1 6.1 fusion.53
  592.2 6.9 all-reduce.6
  599.4 63.2 %all-reduce.4 = (bf16[512]{0:T(512)(128)(2,1)S(1)}, bf16[512]{0:T(512)(128)(2,1)S(1)}, bf16[1536]{0:T(1024)(128)(2,1)S(1)}, bf16[512]{0:T(512)(128)(2,1)S(1)}, bf16[2048]{0:T(1024)(128)(2,1)S(1)}) all-reduce(bf16[512]{0:T(512)(128)(2,1)S(1)} %dynamic-slice.2, ...), channel_id=1, replica_groups=mesh['dp'=16,'mlp'=2] {'dp'}, use_global_device_ids=true, to_apply=%region_16.17 | all-reduce | flops 5120 | bytes 20480 | tf_op jit(solution)/shard_map/psum | solution.py:293
  667.2 157.1 %all-reduce.9.cloned.1.call-done = (bf16[1024,1536]{1,0:T(8,128)(2,1)}, bf16[1024,512]{1,0:T(8,128)(2,1)}, bf16[1024,2048]{1,0:T(8,128)(2,1)}, bf16[2048,1024]{1,0:T(8,128)(2,1)}) async-done(((bf16[1024,1536]{1,0:T(8,128)(2,1)}, bf16[1024,512]{1,0:T(8,128)(2,1)}, bf16[1024,2048]{1,0:T(8,128)(2,1)}, bf16[2048,1024]{1,0:T(8,128)(2,1)}), (bf16[1024,1536]{1,0:T(8,128)(2,1)}, bf16[1024,512]{1,0:T(8,128)(2,1)}, ...) | async-done | bytes 12582928 | tf_op jit(solution)/shard_map/psum | solution.py:289
  824.3 6.8 convert_element_type.175
  (203 shorter events, 151.3 us)
Async XLA Ops:
  7.2 188.6 %copy-start = (bf16[1024,1024]{1,0:T(8,128)(2,1)S(1)}, bf16[1024,1024]{1,0:T(8,128)(2,1)}, u32[]{:S(2)}) copy-start(bf16[1024,1024]{1,0:T(8,128)(2,1)} %param.23) | copy-start | bytes 6291460
  7.2 83.2 %all-gather.6.cloned.1.call-start = ((), (), s32[]{:S(2)}) async-start(), calls=%async_computation.6 | async-start | bytes 5570560 | tf_op jit(solution)/shard_map/all_gather | solution.py:124
  10.2 15.1 %copy-start.17 = (f32[160,8]{1,0:T(8,128)}, f32[160,8]{1,0:T(8,128)S(1)}, u32[]{:S(2)}) copy-start(f32[160,8]{1,0:T(8,128)S(1)} %copy.82) | copy-start | bytes 15364
  31.8 115.8 %all-gather.4.cloned.1.call-start = ((), (), s32[]{:S(2)}) async-start(), calls=%async_computation.5 | async-start | bytes 5570560 | tf_op jit(solution)/shard_map/all_gather | solution.py:125
  33.8 394.1 %reduce-scatter.8.cloned.1.call-start = ((), (), s32[]{:S(2)}) async-start(), calls=%async_computation.8 | async-start | bytes 11141120 | tf_op jit(solution)/shard_map/reduce_scatter | solution.py:246
  155.5 40.2 %copy-start.10 = (bf16[1,1,160,1024]{3,2,1,0:T(8,128)(2,1)S(1)}, bf16[1,1,160,1024]{3,2,1,0:T(8,128)(2,1)}, u32[]{:S(2)}) copy-start(bf16[1,1,160,1024]{3,2,1,0:T(8,128)(2,1)} %param.29) | copy-start | bytes 983044
  203.3 6.6 copy-start.3
  220.1 7.1 copy-start.2
  258.5 6.6 copy-start.3
  275.3 7.1 copy-start.2
  309.6 6.0 copy-start.4
  309.6 189.5 %reduce-scatter.14.cloned.1.call-start = ((), (), s32[]{:S(2)}) async-start(), calls=%async_computation.11 | async-start | bytes 3145728 | tf_op jit(solution)/shard_map/reduce_scatter | solution.py:272
  313.6 235.4 %reduce-scatter.12.cloned.1.call-start = ((), (), s32[]{:S(2)}) async-start(), calls=%async_computation.10 | async-start | bytes 9437184 | tf_op jit(solution)/shard_map/reduce_scatter | solution.py:269
  318.0 7.0 copy-start.16
  442.0 17.9 %copy-start.35 = (f32[2048]{0:T(1024)S(1)}, f32[2048]{0:T(1024)}, u32[]{:S(2)}) copy-start(f32[2048]{0:T(1024)} %param.26) | copy-start | bytes 24580
  442.0 125.8 %reduce-scatter.6.cloned.1.call-start = ((), (), s32[]{:S(2)}) async-start(), calls=%async_computation.7 | async-start | bytes 983040 | tf_op jit(solution)/shard_map/reduce_scatter | solution.py:167
  459.9 5.7 copy-start.21
  459.9 6.8 copy-start.33
  469.1 117.0 %reduce-scatter.10.cloned.1.call-start = ((), (), s32[]{:S(2)}) async-start(), calls=%async_computation.9 | async-start | bytes 983040 | tf_op jit(solution)/shard_map/reduce_scatter | solution.py:185
  478.6 6.5 copy-start.22
  478.6 7.5 copy-start.34
  488.6 335.7 %all-reduce.9.cloned.1.call-start = ((), (), s32[]{:S(2)}) async-start(), calls=%async_computation.12 | async-start | bytes 25165824 | tf_op jit(solution)/shard_map/psum | solution.py:289
  488.6 6.1 copy-start.23
  488.6 6.1 copy-start.38
  549.0 18.8 %copy-start.6 = (bf16[1,1,160,1024]{3,2,1,0:T(8,128)(2,1)S(1)}, bf16[1,1,160,1024]{3,2,1,0:T(8,128)(2,1)}, u32[]{:S(2)}) copy-start(bf16[1,1,160,1024]{3,2,1,0:T(8,128)(2,1)} %param.17) | copy-start | bytes 983044
  549.0 18.8 %copy-start.24 = (f32[1024]{0:T(1024)S(1)}, f32[1024]{0:T(1024)}, u32[]{:S(2)}) copy-start(f32[1024]{0:T(1024)} %param.28) | copy-start | bytes 12292
  549.0 18.8 %copy-start.25 = (f32[1024]{0:T(1024)S(1)}, f32[1024]{0:T(1024)}, u32[]{:S(2)}) copy-start(f32[1024]{0:T(1024)} %param.24) | copy-start | bytes 12292
  549.0 37.1 %copy-start.27 = (f32[160]{0:T(256)S(1)}, f32[160]{0:T(256)}, u32[]{:S(2)}) copy-start(f32[160]{0:T(256)} %copy-done.26) | copy-start | bytes 1924
  549.0 37.1 %copy-start.28 = (f32[1024]{0:T(1024)S(1)}, f32[1024]{0:T(1024)}, u32[]{:S(2)}) copy-start(f32[1024]{0:T(1024)} %param.19) | copy-start | bytes 12292
  549.1 37.1 %copy-start.30 = (f32[160]{0:T(256)S(1)}, f32[160]{0:T(256)}, u32[]{:S(2)}) copy-start(f32[160]{0:T(256)} %copy-done.29) | copy-start | bytes 1924
  663.9 176.9 %copy-start.31 = (f32[512]{0:T(512)}, f32[512]{0:T(512)S(1)}, u32[]{:S(2)}) copy-start(f32[512]{0:T(512)S(1)} %convert_element_type.173) | copy-start | bytes 6148
  824.3 6.8 copy-start.12
  (19 other events, 47.0 us)
Sparse Core Ops, SparseCore 0:
  31.9 58.4 all-gather.5
  93.3 54.3 all-gather.3
  309.7 118.0 reduce-scatter.7
  430.5 38.5 reduce-scatter.13
  471.8 77.1 reduce-scatter.11
  551.7 16.0 reduce-scatter.5
  570.0 16.0 reduce-scatter.9
  591.3 232.9 all-reduce.8
where the time goes:
time: 855 us; the launch traced here: 848 us
  waiting for transfers between devices  442 us (52%)
  matrix products  139 us (16%)
  local copies, waits for them, and re-layouts  107 us (13%)
  blocking collectives  97.3 us (11%)
  other arithmetic  44.8 us (5%)
  between operations  16.8 us (2%)
    psum x1, waiting for transfers between devices, local(): lax.psum(part_qkv.astype(jnp.bfloat16), 'dp').astype(jnp.float32)  157 us
    reduce_scatter x1, waiting for transfers between devices, local(): lax.psum_scatter(grad_kv_sum.astype(jnp.bfloat16), 'dp', scatter_dimensio...  101 us
    psum x1, blocking collectives, local(): lax.psum(part_gain.astype(jnp.bfloat16), 'dp').astype(jnp.float32)  63.2 us
    all_gather x1, waiting for transfers between devices, local(): keys_piece = lax.all_gather(keys_flat, 'dp', axis=0, tiled=True)  52.4 us
    reduce_scatter x1, waiting for transfers between devices, local(): lax.psum_scatter(grad_w_qkv.astype(jnp.bfloat16), 'mlp', scatter_dimensio...  49.9 us
    all_gather x1, waiting for transfers between devices, local(): values_piece = lax.all_gather(values_flat, 'dp', axis=0, tiled=True)  49.4 us
    dynamic_update_slice x4, local copies, waits for them, and re-layouts, local(): lax.scan(back_one_block, grad_query_sum, (keys_piece.reshape(blocks, back...  27.2 us
    unnamed x83, local copies, waits for them, and re-layouts  23 us
  transfers between devices with their start and end apart: 8, of which 7 were waited for; matrix products, arithmetic and copies ran while one was open for 10% of the time, Pallas kernels for 0%

commit v1 on v0

--- a/solution.py
+++ b/solution.py
@@ -1,19 +1,475 @@
+import functools
 import math
 
 import jax
 import jax.numpy as jnp
 from jax import lax
+from jax.experimental import pallas as pl
+from jax.experimental.pallas import tpu as pltpu
 from jax.sharding import PartitionSpec as P
 
 HEADS = 16
 HEAD_DIM = 64
 ROT = 16
-
 
 EPSILON = 1e-05
 ROPE_BASE = 10000.0
 SQRT_HALF = 1.0 / math.sqrt(2.0)
 INV_ROOT_TWO_PI = 1.0 / math.sqrt(2.0 * math.pi)
+
+MESH = pl.DeviceIdType.MESH
+F32 = jnp.float32
+BF16 = jnp.bfloat16
+LANES = 128
+VMEM_BIG = 60 * 1024 * 1024
+
+
+def dot_nn(a, b):
+    return lax.dot_general(a, b, (((1,), (0,)), ((), ())), preferred_element_type=F32)
+
+
+def dot_nt(a, b):
+    return lax.dot_general(a, b, (((1,), (1,)), ((), ())), preferred_element_type=F32)
+
+
+def dot_tn(a, b):
+    return lax.dot_general(a, b, (((0,), (0,)), ((), ())), preferred_element_type=F32)
+
+
+def rotary_tables(positions):
+    lane = jnp.arange(LANES, dtype=jnp.int32) % HEAD_DIM
+    half = ROT // 2
+    frequency = ROPE_BASE ** (-((lane % half).astype(F32) * 2.0 / ROT))
+    angles = positions.astype(F32)[:, None] * frequency[None, :]
+    cosine = jnp.where(lane < ROT, jnp.cos(angles), 1.0)
+    sine = jnp.sin(angles)
+    up = jnp.where(lane < half, -sine, 0.0)
+    down = jnp.where((lane >= half) & (lane < ROT), sine, 0.0)
+    return jnp.stack([cosine, up, down])
+
+
+def rotate_tile(x, tables, sign):
+    half = ROT // 2
+    return (
+        x * tables[0]
+        + pltpu.roll(x, LANES - half, 1) * (tables[1] * sign)
+        + pltpu.roll(x, half, 1) * (tables[2] * sign)
+    )
+
+
+def split_pair(first, second, low):
+    swap_first = pltpu.roll(first, HEAD_DIM, 1)
+    swap_second = pltpu.roll(second, HEAD_DIM, 1)
+    return jnp.where(low, first, swap_second), jnp.where(low, swap_first, second)
+
+
+def project_kernel(
+    x_ref, cot_ref, gain_ref, shift_ref, wq_ref, wk_ref, wv_ref, bq_ref, bk_ref, bv_ref, wo_ref, tab_ref,
+    normed_ref, send_ref,
+):
+    @pl.when(pl.program_id(0) == 0)
+    def _():
+        rows = x_ref[...].astype(F32)
+        centre = jnp.mean(rows, axis=-1, keepdims=True)
+        centred = rows - centre
+        spread = jnp.mean(centred * centred, axis=-1, keepdims=True)
+        unit = centred * lax.rsqrt(spread + EPSILON)
+        normed_ref[...] = (unit * gain_ref[...] + shift_ref[...]).astype(BF16)
+
+    normed = normed_ref[...]
+    q = dot_nn(normed, wq_ref[...]) + bq_ref[...]
+    k = dot_nn(normed, wk_ref[...]) + bk_ref[...]
+    v = dot_nn(normed, wv_ref[...]) + bv_ref[...]
+    grad_att = dot_nt(cot_ref[...], wo_ref[...])
+    tables = [tab_ref[i] for i in range(3)]
+    low = lax.broadcasted_iota(jnp.int32, (x_ref.shape[0], LANES), 1) < HEAD_DIM
+    for tile in range(q.shape[1] // LANES):
+        cols = slice(tile * LANES, (tile + 1) * LANES)
+        q_tile = rotate_tile(q[:, cols], tables, 1.0)
+        k_tile = rotate_tile(k[:, cols], tables, 1.0)
+        qk = split_pair(q_tile, k_tile, low)
+        vg = split_pair(v[:, cols], grad_att[:, cols], low)
+        for side in range(2):
+            send_ref[2 * tile + side, :, :LANES] = qk[side].astype(BF16)
+            send_ref[2 * tile + side, :, LANES:] = vg[side].astype(BF16)
+
+
+def project(x, cot, gain, shift, w_qkv, b_qkv, w_out, tables):
+    tok, width = x.shape
+    group = 256
+    steps = width // group
+    heads_step = group // HEAD_DIM
+    const = lambda shape: pl.BlockSpec(shape, lambda g: (0,) * len(shape))
+    w_spec = lambda part: pl.BlockSpec((width, group), lambda g: (0, part * steps + g))
+    b_spec = lambda part: pl.BlockSpec((1, group), lambda g: (0, part * steps + g))
+    return pl.pallas_call(
+        project_kernel,
+        grid=(steps,),
+        out_shape=(
+            jax.ShapeDtypeStruct((tok, width), BF16),
+            jax.ShapeDtypeStruct((HEADS, tok, 4 * HEAD_DIM), BF16),
+        ),
+        in_specs=[
+            const((tok, width)), const((tok, width)), const((1, width)), const((1, width)),
+            w_spec(0), w_spec(1), w_spec(2), b_spec(0), b_spec(1), b_spec(2),
+            pl.BlockSpec((group, width), lambda g: (g, 0)),
+            const((3, tok, LANES)),
+        ],
+        out_specs=(
+            const((tok, width)),
+            pl.BlockSpec((heads_step, tok, 4 * HEAD_DIM), lambda g: (g, 0, 0)),
+        ),
+        name="project",
+    )(x, cot, gain, shift, w_qkv, w_qkv, w_qkv, b_qkv, b_qkv, b_qkv, w_out, tables)
+
+
+def exchange_kernel(count, peers, blocks, *refs):
+    heads_in, rest = refs[0], refs[1:]
+    pairs_in, rest = rest[:count], rest[count:]
+    heads_out, rest = rest[0], rest[1:]
+    pairs_out, rest = rest[:count], rest[count:]
+    head_send, head_recv, pair_send, pair_recv, local_sem = rest
+    me = lax.axis_index("dp")
+    other = 1 - lax.axis_index("mlp")
+    barrier = pltpu.get_barrier_semaphore()
+    for step in range(1, peers):
+        pl.semaphore_signal(barrier, inc=1, device_id={"dp": lax.rem(me + step, peers)}, device_id_type=MESH)
+    if count:
+        pl.semaphore_signal(barrier, inc=1, device_id={"mlp": other}, device_id_type=MESH)
+    pl.semaphore_wait(barrier, peers - 1 + (1 if count else 0))
+    copies = []
+    for i in range(count):
+        copies.append(
+            pltpu.make_async_remote_copy(
+                src_ref=pairs_in[i], dst_ref=pairs_out[i], send_sem=pair_send.at[i], recv_sem=pair_recv.at[i],
+                device_id={"mlp": other}, device_id_type=MESH,
+            )
+        )
+    for step in range(1, peers):
+        target = lax.rem(me + step, peers)
+        copies.append(
+            pltpu.make_async_remote_copy(
+                src_ref=heads_in.at[target], dst_ref=heads_out.at[me],
+                send_sem=head_send.at[step], recv_sem=head_recv.at[step],
+                device_id={"dp": target}, device_id_type=MESH,
+            )
+        )
+    for copy in copies:
+        copy.start()
+    own = pltpu.make_async_copy(heads_in.at[me], heads_out.at[me], local_sem)
+    own.start()
+    own.wait()
+    for copy in copies:
+        copy.wait()
+
+
+def exchange(heads, pairs, collective):
+    count = len(pairs)
+    peers = heads.shape[0]
+    any_spec = pl.BlockSpec(memory_space=pl.ANY)
+    out = pl.pallas_call(
+        functools.partial(exchange_kernel, count, peers, None),
+        out_shape=(jax.ShapeDtypeStruct(heads.shape, heads.dtype),)
+        + tuple(jax.ShapeDtypeStruct(p.shape, p.dtype) for p in pairs),
+        in_specs=[any_spec] * (1 + count),
+        out_specs=(any_spec,) * (1 + count),
+        scratch_shapes=[
+            pltpu.SemaphoreType.DMA((peers,)),
+            pltpu.SemaphoreType.DMA((peers,)),
+            pltpu.SemaphoreType.DMA((max(count, 1),)),
+            pltpu.SemaphoreType.DMA((max(count, 1),)),
+            pltpu.SemaphoreType.DMA,
+        ],
+        compiler_params=pltpu.CompilerParams(collective_id=collective, has_side_effects=True),
+        name="exchange" + str(collective),
+    )(heads, *pairs)
+    return out[0], out[1:]
+
+
+def swap_kernel(count, *refs):
+    ins, outs = refs[:count], refs[count : 2 * count]
+    send, recv = refs[2 * count :]
+    other = 1 - lax.axis_index("mlp")
+    barrier = pltpu.get_barrier_semaphore()
+    pl.semaphore_signal(barrier, inc=1, device_id={"mlp": other}, device_id_type=MESH)
+    pl.semaphore_wait(barrier, 1)
+    copies = [
+        pltpu.make_async_remote_copy(
+            src_ref=ins[i], dst_ref=outs[i], send_sem=send.at[i], recv_sem=recv.at[i],
+            device_id={"mlp": other}, device_id_type=MESH,
+        )
+        for i in range(count)
+    ]
+    for copy in copies:
+        copy.start()
+    for copy in copies:
+        copy.wait()
+
+
+def swap(arrays, collective):
+    count = len(arrays)
+    any_spec = pl.BlockSpec(memory_space=pl.ANY)
+    return pl.pallas_call(
+        functools.partial(swap_kernel, count),
+        out_shape=tuple(jax.ShapeDtypeStruct(a.shape, a.dtype) for a in arrays),
+        in_specs=[any_spec] * count,
+        out_specs=(any_spec,) * count,
+        scratch_shapes=[pltpu.SemaphoreType.DMA((count,)), pltpu.SemaphoreType.DMA((count,))],
+        compiler_params=pltpu.CompilerParams(collective_id=collective, has_side_effects=True),
+        name="swap" + str(collective),
+    )(*arrays)
+
+
+def attention_kernel(
+    tile, order_ref, in_ref, out_ref,
+    q_nat, k_nat, v_nat, k_tr, v_tr, g_tr, probs, kv_grad, aq_out,
+):
+    spans, tok, _ = in_ref.shape
+    length = spans * tok
+    blocks = length // tile
+    scale = 1.0 / math.sqrt(HEAD_DIM)
+    zeros = jnp.zeros((tok, HEAD_DIM), BF16)
+
+    def gather(place, carry):
+        span = order_ref[place]
+        rows = pl.ds(pl.multiple_of(place * tok, tok), tok)
+        data = in_ref[span]
+        q_nat[rows, :] = jnp.concatenate([data[:, :HEAD_DIM] * jnp.asarray(scale, BF16), zeros], axis=1)
+        k_nat[rows, :] = data[:, HEAD_DIM : 2 * HEAD_DIM]
+        v_nat[rows, :] = data[:, 2 * HEAD_DIM : 3 * HEAD_DIM]
+        return carry
+
+    lax.fori_loop(0, spans, gather, 0)
+
+    def gather_grad(place, carry):
+        span = order_ref[place]
+        rows = pl.ds(pl.multiple_of(place * tok, tok), tok)
+        g_nat_rows = in_ref[span][:, 3 * HEAD_DIM :]
+        aq_out[rows, :HEAD_DIM] = g_nat_rows
+        return carry
+
+    lax.fori_loop(0, spans, gather_grad, 0)
+
+    def flip(block, carry):
+        rows = pl.ds(pl.multiple_of(block * tile, tile), tile)
+        k_tr[:, rows] = k_nat[rows, :].T
+        v_tr[:, rows] = v_nat[rows, :].T
+        g_tr[:, rows] = aq_out[rows, :HEAD_DIM].T
+        kv_grad[rows, :] = jnp.zeros((tile, 2 * HEAD_DIM), F32)
+        return carry
+
+    lax.fori_loop(0, blocks, flip, 0)
+
+    key_row = lax.broadcasted_iota(jnp.int32, (tile, tile), 0)
+    query_col = lax.broadcasted_iota(jnp.int32, (tile, tile), 1)
+    causal = key_row <= query_col
+    pad = jnp.zeros((tile, HEAD_DIM), BF16)
+
+    def query_block(block, carry):
+        q_rows = pl.ds(pl.multiple_of(block * tile, tile), tile)
+        queries_pad = q_nat[q_rows, :]
+        queries = queries_pad[:, :HEAD_DIM]
+
+        def forward(j, state, masked):
+            mixed, totals = state
+            rows = pl.ds(pl.multiple_of(j * tile, tile), tile)
+            prob = jnp.exp(dot_nt(k_nat[rows, :], queries))
+            if masked:
+                prob = jnp.where(causal, prob, 0.0)
+            probs[rows, :] = prob
+            mixed = mixed + dot_nn(v_tr[:, rows], prob.astype(BF16))
+            totals = totals + jnp.sum(prob.reshape(tile // 8, 8, tile), axis=0)
+            return mixed, totals
+
+        state = (jnp.zeros((HEAD_DIM, tile), F32), jnp.zeros((8, tile), F32))
+        state = lax.fori_loop(0, block, lambda j, s: forward(j, s, False), state)
+        mixed, totals = forward(block, state, True)
+        totals = jnp.sum(totals, axis=0, keepdims=True)
+        attended = mixed / totals
+        grad_att = g_tr[:, q_rows].astype(F32)
+        grad_mixed = (grad_att / totals).astype(BF16)
+        grad_totals = (-jnp.sum(grad_att * attended, axis=0, keepdims=True) / totals).astype(BF16).astype(F32)
+        grad_pad = jnp.concatenate([pad, grad_mixed.T], axis=1)
+
+        def backward(j, grad_q):
+            rows = pl.ds(pl.multiple_of(j * tile, tile), tile)
+            prob = probs[rows, :]
+            grad_scores = (prob * (dot_nn(v_nat[rows, :], grad_mixed) + grad_totals)).astype(BF16)
+            kv_grad[rows, :] += dot_nn(grad_scores, queries_pad) + dot_nn(prob.astype(BF16), grad_pad)
+            return grad_q + dot_nn(k_tr[:, rows], grad_scores)
+
+        grad_q = lax.fori_loop(0, block + 1, backward, jnp.zeros((HEAD_DIM, tile), F32))
+        aq_out[q_rows, :] = jnp.concatenate([attended, grad_q * scale], axis=0).T.astype(BF16)
+        return carry
+
+    lax.fori_loop(0, blocks, query_block, 0)
+
+    def scatter(place, carry):
+        span = order_ref[place]
+        rows = pl.ds(pl.multiple_of(place * tok, tok), tok)
+        out_ref[span, :, : 2 * HEAD_DIM] = aq_out[rows, :]
+        out_ref[span, :, 2 * HEAD_DIM :] = kv_grad[rows, :].astype(BF16)
+        return carry
+
+    lax.fori_loop(0, spans, scatter, 0)
+
+
+def attention(heads, order):
+    spans, tok, width = heads.shape
+    length = spans * tok
+    tile = 256
+    vmem = pl.BlockSpec(memory_space=pltpu.VMEM)
+    return pl.pallas_call(
+        functools.partial(attention_kernel, tile),
+        out_shape=jax.ShapeDtypeStruct(heads.shape, BF16),
+        in_specs=[pl.BlockSpec(memory_space=pltpu.SMEM), vmem],
+        out_specs=vmem,
+        scratch_shapes=[
+            pltpu.VMEM((length, 2 * HEAD_DIM), BF16),
+            pltpu.VMEM((length, HEAD_DIM), BF16),
+            pltpu.VMEM((length, HEAD_DIM), BF16),
+            pltpu.VMEM((HEAD_DIM, length), BF16),
+            pltpu.VMEM((HEAD_DIM, length), BF16),
+            pltpu.VMEM((HEAD_DIM, length), BF16),
+            pltpu.VMEM((length, tile), F32),
+            pltpu.VMEM((length, 2 * HEAD_DIM), F32),
+            pltpu.VMEM((length, 2 * HEAD_DIM), BF16),
+        ],
+        compiler_params=pltpu.CompilerParams(vmem_limit_bytes=VMEM_BIG),
+        name="attention",
+    )(order, heads)
+
+
+def finish_kernel(
+    heads_ref, x_ref, cot_ref, gain_ref, wqkv_ref, wout_ref, bias_ref, mlp_a, mlp_b, gn_a, gn_b, tab_ref,
+    out_ref, grad_in_ref, att_ref, gproj_ref, small_ref, bqkv_ref,
+):
+    tok, width = x_ref.shape
+    tables = [tab_ref[i] for i in range(3)]
+    low = lax.broadcasted_iota(jnp.int32, (tok, LANES), 1) < HEAD_DIM
+    for pair in range(HEADS // 2):
+        cols = slice(pair * LANES, (pair + 1) * LANES)
+        even, odd = heads_ref[2 * pair].astype(F32), heads_ref[2 * pair + 1].astype(F32)
+        att, gq = split_pair(even[:, :LANES], odd[:, :LANES], low)
+        gk, gv = split_pair(even[:, LANES:], odd[:, LANES:], low)
+        att_ref[:, cols] = att.astype(BF16)
+        gproj_ref[:, pair * LANES : (pair + 1) * LANES] = rotate_tile(gq, tables, -1.0).astype(BF16)
+        gproj_ref[:, width + pair * LANES : width + (pair + 1) * LANES] = rotate_tile(gk, tables, -1.0).astype(BF16)
+        gproj_ref[:, 2 * width + pair * LANES : 2 * width + (pair + 1) * LANES] = gv.astype(BF16)
+    rows = x_ref[...].astype(F32)
+    cot = cot_ref[...].astype(F32)
+    attn = dot_nn(att_ref[...], wout_ref[...])
+    branch = mlp_a[...].astype(F32) + mlp_b[...].astype(F32)
+    out_ref[...] = (rows + attn + branch + bias_ref[...]).astype(BF16)
+    grad_normed = dot_nt(gproj_ref[...], wqkv_ref[...]) + gn_a[...].astype(F32) + gn_b[...].astype(F32)
+    centre = jnp.mean(rows, axis=-1, keepdims=True)
+    centred = rows - centre
+    inv = lax.rsqrt(jnp.mean(centred * centred, axis=-1, keepdims=True) + EPSILON)
+    unit = centred * inv
+    small_ref[0:1, :] = jnp.sum(grad_normed * unit, axis=0, keepdims=True)
+    small_ref[1:2, :] = jnp.sum(grad_normed, axis=0, keepdims=True)
+    small_ref[2:3, :] = jnp.sum(cot, axis=0, keepdims=True)
+    bqkv_ref[...] = jnp.sum(gproj_ref[...].astype(F32), axis=0, keepdims=True)
+    grad_unit = grad_normed * gain_ref[...]
+    grad_in_ref[...] = cot + inv * (
+        grad_unit
+        - jnp.mean(grad_unit, axis=-1, keepdims=True)
+        - unit * jnp.mean(grad_unit * unit, axis=-1, keepdims=True)
+    )
+
+
+def finish(heads, x, cot, gain, w_qkv, w_out, bias, mlp_parts, gn_parts, tables):
+    tok, width = x.shape
+    vmem = pl.BlockSpec(memory_space=pltpu.VMEM)
+    return pl.pallas_call(
+        finish_kernel,
+        out_shape=(
+            jax.ShapeDtypeStruct((tok, width), BF16),
+            jax.ShapeDtypeStruct((tok, width), F32),
+            jax.ShapeDtypeStruct((tok, width), BF16),
+            jax.ShapeDtypeStruct((tok, 3 * width), BF16),
+            jax.ShapeDtypeStruct((8, width), F32),
+            jax.ShapeDtypeStruct((1, 3 * width), F32),
+        ),
+        in_specs=[vmem] * 12,
+        out_specs=(vmem,) * 6,
+        compiler_params=pltpu.CompilerParams(vmem_limit_bytes=VMEM_BIG),
+        name="finish",
+    )(heads, x, cot, gain, w_qkv, w_out, bias, *mlp_parts, *gn_parts, tables)
+
+
+def by_heads(
+    block_input, span_offset, ln_gain, ln_bias, w_qkv, b_qkv, w_out, b_out, w_up, b_up, w_down, b_down, cotangent
+):
+    tok, width = block_input.shape[2:]
+    spans = span_offset.shape[0]
+    span_here = lax.axis_index("dp")
+    seq_here = lax.axis_index("mlp")
+    offsets = lax.dynamic_index_in_dim(span_offset, seq_here, axis=1, keepdims=False)
+    places = jnp.arange(spans, dtype=jnp.int32)
+    order = jnp.sum(jnp.where(offsets[None, :] == places[:, None], places[None, :], 0), axis=1)
+    offset_here = lax.dynamic_index_in_dim(offsets, span_here, axis=0, keepdims=False)
+    tables = rotary_tables(offset_here * tok + jnp.arange(tok, dtype=jnp.int32))
+    x, cot = block_input[0, 0], cotangent[0, 0]
+    gain, shift = ln_gain[None], ln_bias[None]
+
+    normed, send = project(x, cot, gain, shift, w_qkv, b_qkv[None], w_out, tables)
+    heads, (normed_peer, cot_peer) = exchange(send, (normed, cot), 0)
+
+    normed_all = jnp.concatenate([normed, normed_peer])
+    cot_all = jnp.concatenate([cot, cot_peer])
+    up = dot_nn(normed_all, w_up) + b_up
+    erf_part = 0.5 * (1.0 + lax.erf(up * SQRT_HALF))
+    activated = (up * erf_part).astype(BF16)
+    slope = erf_part + up * jnp.exp(-0.5 * up * up) * INV_ROOT_TWO_PI
+    grad_up = (dot_nt(cot_all, w_down) * slope).astype(BF16)
+    mlp_part = dot_nn(activated, w_down).astype(BF16)
+    gn_part = dot_nt(grad_up, w_up).astype(BF16)
+    grad_w_down = dot_tn(activated, cot_all).astype(BF16)
+    grad_w_up = dot_tn(normed_all, grad_up).astype(BF16)
+    grad_b_up = jnp.sum(grad_up.astype(F32), axis=0).astype(BF16)
+
+    done = attention(heads, order)
+    back, (mlp_other, gn_other) = exchange(done, (mlp_part[tok:], gn_part[tok:]), 1)
+    output, grad_input, attended, grad_project, small, grad_b_qkv = finish(
+        back, x, cot, gain, w_qkv, w_out, (b_out + b_down)[None],
+        (mlp_part[:tok], mlp_other), (gn_part[:tok], gn_other), tables,
+    )
+    third = 3 * width // 2
+    gp_here = lax.dynamic_slice_in_dim(grad_project, seq_here * third, third, axis=1)
+    gp_give = lax.dynamic_slice_in_dim(grad_project, (1 - seq_here) * third, third, axis=1)
+    att_peer, gp_peer = swap((attended, gp_give), 2)
+    cot_cols = lax.dynamic_slice_in_dim(cot_all, seq_here * (width // 2), width // 2, axis=1)
+    grad_w_qkv = dot_tn(normed_all, jnp.concatenate([gp_here, gp_peer])).astype(BF16)
+    grad_w_out = dot_tn(jnp.concatenate([attended, att_peer]), cot_cols).astype(BF16)
+
+    everyone = ("dp", "mlp")
+    vec = jnp.concatenate([small[0], small[1], small[2], grad_b_qkv[0]])
+    vec, b_up_sum, s_qkv, s_out, s_up, s_down = (
+        lax.psum(vec, everyone),
+        lax.psum(grad_b_up, "dp"),
+        lax.psum(grad_w_qkv, "dp"),
+        lax.psum(grad_w_out, "dp"),
+        lax.psum(grad_w_up, "dp"),
+        lax.psum(grad_w_down, "dp"),
+    )
+    half = width // 2
+    piece = lambda start, size: lax.dynamic_slice_in_dim(vec, start + seq_here * size, size)
+    bias_sum = piece(2 * width, half)
+    return (
+        output.reshape(1, 1, tok, width),
+        grad_input.reshape(1, 1, tok, width),
+        piece(0, half),
+        piece(width, half),
+        s_qkv.astype(F32),
+        piece(3 * width, third),
+        s_out.astype(F32),
+        bias_sum,
+        s_up.astype(F32),
+        b_up_sum.astype(F32),
+        s_down.astype(F32),
+        bias_sum,
+    )
 
 
 def rotate(values, positions, sign_factor):
@@ -313,8 +769,9 @@
 
 
 def solution(mesh):
+    fits = mesh.shape["dp"] == HEADS and mesh.shape["mlp"] == 2
     return jax.shard_map(
-        local,
+        by_heads if fits else local,
         mesh=mesh,
         in_specs=(
             P("dp", "mlp", None, None),

time: 855 us -> 453 us (0.53)
  waiting for transfers between devices: 442 us -> 158 us
  Pallas kernels: 0 us -> 143 us
  matrix products: 139 us -> 25.6 us
  local copies, waits for them, and re-layouts: 107 us -> 10.6 us
  other arithmetic: 44.8 us -> 19.4 us
  blocking collectives: 97.3 us -> 81.1 us
    reduce_scatter x5 -> x0, waiting for transfers between devices: 183 us -> none  [the longest x1 101 us: local(): lax.psum_scatter(grad_kv_sum.astype(jnp.bfloat16), 'dp', scatter_dimensio...]
    pallas_call x0 -> x6, Pallas kernels: none -> 143 us  [the longest x2 61.4 us: exchange(): pl.pallas_call(functools.partial(exchange_kernel, count, peers, None), ou...]
    dot_general x26 -> x8, matrix products: 139 us -> 25.6 us  [the longest x4 15.1 us: dot_tn(): lax.dot_general(a, b, (((0,), (0,)), ((), ())), preferred_element_type=F32)]
    all_gather x2 -> x0, waiting for transfers between devices: 102 us -> none  [the longest x1 52.4 us: local(): keys_piece = lax.all_gather(keys_flat, 'dp', axis=0, tiled=True)]
    dynamic_update_slice x4 -> x0, local copies, waits for them, and re-layouts: 27.2 us -> none  [local(): lax.scan(back_one_block, grad_query_sum, (keys_piece.reshape(blocks, back...]
    all_gather x2 -> x0, blocking collectives: 27.2 us -> none  [the longest x1 17.8 us: local(): normed_all = lax.all_gather(normed, 'mlp', axis=0, tiled=True)]
    unnamed x83 -> x32, local copies, waits for them, and re-layouts: 23 us -> 1.65 us
    psum x1 -> x2, blocking collectives: 63.2 us -> 81.1 us  [the longest x1 48.7 us: by_heads(): lax.psum(vec, everyone)]
  transfers between devices with their start and end apart: 8 -> 1, of which waited for: 7 -> 1; matrix products, arithmetic and copies ran while one was open for 10% -> 1% of each run, Pallas kernels for 0% -> 0%
where the time goes in v1:
time: 453 us; the launch traced here: 452 us
  waiting for transfers between devices  158 us (35%)
  Pallas kernels  143 us (32%)
  blocking collectives  81.1 us (18%)
  matrix products  25.6 us (6%)
  other arithmetic  19.4 us (4%)
  between operations  15 us (3%)
  local copies, waits for them, and re-layouts  10.6 us (2%)
    psum x1, waiting for transfers between devices, by_heads(): lax.psum(grad_w_qkv, 'dp')  158 us
    pallas_call x2, Pallas kernels, exchange(): pl.pallas_call(functools.partial(exchange_kernel, count, peers, None), ou...  61.4 us
    psum x1, blocking collectives, by_heads(): lax.psum(vec, everyone)  48.7 us
    pallas_call x1, Pallas kernels, attention(): pl.pallas_call(functools.partial(attention_kernel, tile), out_shape=jax.S...  45.2 us
    psum x1, blocking collectives, by_heads(): lax.psum(grad_b_up, 'dp')  32.4 us
    pallas_call x1, Pallas kernels, swap(): pl.pallas_call(functools.partial(swap_kernel, count), out_shape=tuple((ja...  20 us
    dot_general x4, matrix products, dot_tn(): lax.dot_general(a, b, (((0,), (0,)), ((), ())), preferred_element_type=F32)  15.1 us
  transfers between devices with their start and end apart: 1, of which 1 were waited for; matrix products, arithmetic and copies ran while one was open for 1% of the time, Pallas kernels for 0%

profile of v1, /device:TPU:0, one launch (start us, length us, event | category | flops | bytes accessed | tf_op | source)
XLA Modules:
  0.0 452.4 jit_solution(17190738785532551039)
XLA Ops:
  7.3 0.7 fusion.18
  8.0 1.3 dynamic_slice.30
  10.3 0.7 pad_maximum_fusion.3.tab_ref
  11.0 7.1 %project.1 = (bf16[160,1024]{1,0:T(8,128)(2,1)}, bf16[16,160,256]{2,1,0:T(8,128)(2,1)}) custom-call(bf16[160,1024]{1,0:T(8,128)(2,1)} %bitcast.32, bf16[160,1024]{1,0:T(8,128)(2,1)} %bitcast.26, f32[1,1024]{1,0:T(1,128)} %bitcast.37, f32[1,1024]{1,0:T(1,128)} %bitcast.44, bf16[1024,3072]{1,0:T(8,128)(2,1)} %wqkv_ref.1, bf16[1024,3072]{1,0:T(8,128)(2,1)} %wqkv_ref.1, ...), custom_call_target="tpu_custom_call" | custom-call | tf_op jit(solution)/shard_map/project/pallas_call | solution.py:105
  18.1 1.0 constant_dynamic-update-slice_fusion.1
  19.1 28.4 %exchange0.1 = (bf16[16,160,256]{2,1,0:T(8,128)(2,1)}, bf16[160,1024]{1,0:T(8,128)(2,1)}, bf16[160,1024]{1,0:T(8,128)(2,1)}) custom-call(bf16[16,160,256]{2,1,0:T(8,128)(2,1)} %get-tuple-element.28.refs_0_, bf16[160,1024]{1,0:T(8,128)(2,1)} %get-tuple-element.29.refs_1_, bf16[160,1024]{1,0:T(8,128)(2,1)} %bitcast.27), custom_call_target="tpu_custom_call" | custom-call | tf_op jit(solution)/shard_map/exchange0/pallas_call | solution.py:170
  47.5 1.0 constant_dynamic-update-slice_fusion
  48.5 3.8 multiply_convert_fusion
  52.4 3.6 fusion.32
  56.0 1.6 convolution_convert_fusion.4
  57.6 4.4 convolution_convert_fusion.1
  62.0 1.6 convolution_convert_fusion.5
  63.6 4.4 convolution_convert_fusion
  68.0 0.9 fusion.28
  68.9 0.9 fusion.29
  70.4 45.2 %attention.1.refs_0_ = bf16[16,160,256]{2,1,0:T(8,128)(2,1)} custom-call(s32[16]{0:T(128)} %select_reduce_fusion.order_ref, bf16[16,160,256]{2,1,0:T(8,128)(2,1)} %get-tuple-element.30.in_ref), custom_call_target="tpu_custom_call" | custom-call | tf_op jit(solution)/shard_map/attention/pallas_call | solution.py:322
  116.2 33.0 %exchange1.1 = (bf16[16,160,256]{2,1,0:T(8,128)(2,1)}, bf16[160,1024]{1,0:T(8,128)(2,1)}, bf16[160,1024]{1,0:T(8,128)(2,1)}) custom-call(bf16[16,160,256]{2,1,0:T(8,128)(2,1)} %attention.1.refs_0_, bf16[160,1024]{1,0:T(8,128)(2,1)} %get-tuple-element.53.refs_1_, bf16[160,1024]{1,0:T(8,128)(2,1)} %get-tuple-element.51.refs_2_), custom_call_target="tpu_custom_call" | custom-call | tf_op jit(solution)/shard_map/exchange1/pallas_call | solution.py:170
  149.2 8.9 %finish.1 = (bf16[160,1024]{1,0:T(8,128)(2,1)}, f32[160,1024]{1,0:T(8,128)}, bf16[160,1024]{1,0:T(8,128)(2,1)}, bf16[160,3072]{1,0:T(8,128)(2,1)}, f32[8,1024]{1,0:T(8,128)}, /*index=5*/f32[1,3072]{1,0:T(1,128)}) custom-call(bf16[16,160,256]{2,1,0:T(8,128)(2,1)} %get-tuple-element.33.heads_ref, bf16[160,1024]{1,0:T(8,128)(2,1)} %bitcast.33, ...), custom_call_target="tpu_custom_call" | custom-call | tf_op jit(solution)/shard_map/finish/pallas_call | solution.py:384
  158.1 2.1 constant_dynamic-slice_fusion.1
  160.2 20.0 %swap2.1 = (bf16[160,1024]{1,0:T(8,128)(2,1)}, bf16[160,1536]{1,0:T(8,128)(2,1)}) custom-call(bf16[160,1024]{1,0:T(8,128)(2,1)} %get-tuple-element.41.refs_0_, bf16[160,1536]{1,0:T(8,128)(2,1)} %get-tuple-element.49.refs_1_), custom_call_target="tpu_custom_call" | custom-call | tf_op jit(solution)/shard_map/swap2/pallas_call | solution.py:212
  180.2 2.8 convolution_convert_fusion.3
  183.0 3.5 convolution_convert_fusion.2
  186.5 0.9 fusion.30
  187.4 48.7 %psum.42 = f32[6144]{0:T(1024)S(1)} all-reduce(f32[6144]{0:T(1024)S(1)} %pad_maximum_fusion.4), channel_id=1, replica_groups=mesh['dp'=16,'mlp'=2] {'dp','mlp'}, use_global_device_ids=true, to_apply=%region_1.2 | all-reduce | flops 6144 | bytes 49152 | tf_op jit(solution)/shard_map/psum | solution.py:449
  236.1 0.7 dynamic_slice.35
  236.8 0.7 fusion.31
  237.4 32.4 %psum.46 = bf16[2048]{0:T(1024)(128)(2,1)S(1)} all-reduce(bf16[2048]{0:T(1024)(128)(2,1)S(1)} %get-tuple-element.65), channel_id=1, replica_groups=mesh['dp'=16,'mlp'=2] {'dp'}, use_global_device_ids=true, to_apply=%region_6.7 | all-reduce | flops 2048 | bytes 8192 | tf_op jit(solution)/shard_map/psum | solution.py:450
  270.4 158.1 %all-reduce.3.cloned.1.call-done = (bf16[1024,1536]{1,0:T(8,128)(2,1)}, bf16[1024,512]{1,0:T(8,128)(2,1)}, bf16[1024,2048]{1,0:T(8,128)(2,1)}, bf16[2048,1024]{1,0:T(8,128)(2,1)}) async-done(((bf16[1024,1536]{1,0:T(8,128)(2,1)}, bf16[1024,512]{1,0:T(8,128)(2,1)}, bf16[1024,2048]{1,0:T(8,128)(2,1)}, bf16[2048,1024]{1,0:T(8,128)(2,1)}), (bf16[1024,1536]{1,0:T(8,128)(2,1)}, bf16[1024,512]{1,0:T(8,128)(2,1)}, ...) | async-done | bytes 12582928 | tf_op jit(solution)/shard_map/psum | solution.py:451
  428.5 6.8 %convert_element_type.66 = f32[1024,2048]{1,0:T(8,128)} convert(bf16[1024,2048]{1,0:T(8,128)(2,1)} %get-tuple-element.46) | non-fusion elementwise | flops 2097152 | bytes 12582912 | tf_op jit(solution)/shard_map/convert_element_type | solution.py:468
  435.3 4.4 convert_element_type.69
  439.8 3.6 convert_element_type.62
  443.3 1.6 convert_element_type.64
  (42 shorter events, 2.9 us)
Async XLA Ops:
  7.2 421.3 %all-reduce.3.cloned.1.call-start = ((), (), s32[]{:S(2)}) async-start(), calls=%async_computation | async-start | bytes 25165824 | tf_op jit(solution)/shard_map/psum | solution.py:451
  18.1 30.4 %copy-start.14 = (f32[2048]{0:T(1024)S(1)}, f32[2048]{0:T(1024)}, u32[]{:S(2)}) copy-start(f32[2048]{0:T(1024)} %param.22) | copy-start | bytes 24580
  48.5 3.8 copy-start.2
  48.5 3.8 copy-start.11
  48.5 3.8 copy-start.13
  52.3 3.7 copy-start.10
  68.0 47.6 %copy-start.8 = (f32[1024]{0:T(1024)S(1)}, f32[1024]{0:T(1024)}, u32[]{:S(2)}) copy-start(f32[1024]{0:T(1024)} %param.20) | copy-start | bytes 12292
  68.0 47.6 %copy-start.9 = (f32[1024]{0:T(1024)S(1)}, f32[1024]{0:T(1024)}, u32[]{:S(2)}) copy-start(f32[1024]{0:T(1024)} %param.24) | copy-start | bytes 12292
  158.1 22.2 %copy-start.3 = (bf16[1,1,160,1024]{3,2,1,0:T(8,128)(2,1)S(1)}, bf16[1,1,160,1024]{3,2,1,0:T(8,128)(2,1)}, u32[]{:S(2)}) copy-start(bf16[1,1,160,1024]{3,2,1,0:T(8,128)(2,1)} %param.25) | copy-start | bytes 983044
  158.1 22.2 %copy-start.5 = (bf16[160,1024]{1,0:T(8,128)(2,1)S(1)}, bf16[160,1024]{1,0:T(8,128)(2,1)}, u32[]{:S(2)}) copy-start(bf16[160,1024]{1,0:T(8,128)(2,1)} %get-tuple-element.41.refs_0_) | copy-start | bytes 983044
  180.2 2.8 copy-start.12
  186.5 0.9 copy-start.6
  237.4 207.5 %copy-start.7 = (f32[512]{0:T(512)}, f32[512]{0:T(512)S(1)}, u32[]{:S(2)}) copy-start(f32[512]{0:T(512)S(1)} %get-tuple-element.92) | copy-start | bytes 6148
  428.5 6.8 %copy-start = (bf16[2048,1024]{1,0:T(8,128)(2,1)S(1)}, bf16[2048,1024]{1,0:T(8,128)(2,1)}, u32[]{:S(2)}) copy-start(bf16[2048,1024]{1,0:T(8,128)(2,1)} %get-tuple-element.47) | copy-start | bytes 12582916
  435.3 4.4 copy-start.1
  439.8 3.6 copy-start.4
Sparse Core Ops, SparseCore 0:
  186.6 241.8 all-reduce.2

commit v2 on v1

--- a/solution.py
+++ b/solution.py
@@ -342,7 +342,7 @@
 
 def finish_kernel(
     heads_ref, x_ref, cot_ref, gain_ref, wqkv_ref, wout_ref, bias_ref, mlp_a, mlp_b, gn_a, gn_b, tab_ref,
-    out_ref, grad_in_ref, att_ref, gproj_ref, small_ref, bqkv_ref,
+    out_ref, grad_in_ref, att_ref, gproj_ref, small_ref,
 ):
     tok, width = x_ref.shape
     tables = [tab_ref[i] for i in range(3)]
@@ -369,7 +369,10 @@
     small_ref[0:1, :] = jnp.sum(grad_normed * unit, axis=0, keepdims=True)
     small_ref[1:2, :] = jnp.sum(grad_normed, axis=0, keepdims=True)
     small_ref[2:3, :] = jnp.sum(cot, axis=0, keepdims=True)
-    bqkv_ref[...] = jnp.sum(gproj_ref[...].astype(F32), axis=0, keepdims=True)
+    for part in range(3):
+        part_cols = slice(part * width, (part + 1) * width)
+        small_ref[3 + part : 4 + part, :] = jnp.sum(gproj_ref[:, part_cols].astype(F32), axis=0, keepdims=True)
+    small_ref[6:8, :] = jnp.zeros((2, width), F32)
     grad_unit = grad_normed * gain_ref[...]
     grad_in_ref[...] = cot + inv * (
         grad_unit
@@ -389,13 +392,335 @@
             jax.ShapeDtypeStruct((tok, width), BF16),
             jax.ShapeDtypeStruct((tok, 3 * width), BF16),
             jax.ShapeDtypeStruct((8, width), F32),
-            jax.ShapeDtypeStruct((1, 3 * width), F32),
         ),
         in_specs=[vmem] * 12,
-        out_specs=(vmem,) * 6,
+        out_specs=(vmem,) * 5,
         compiler_params=pltpu.CompilerParams(vmem_limit_bytes=VMEM_BIG),
         name="finish",
     )(heads, x, cot, gain, w_qkv, w_out, bias, *mlp_parts, *gn_parts, tables)
+
+
+CHUNK = 64
+
+
+def feed_forward_kernel(
+    normed_a, normed_b, cot_a, cot_b, wup_ref, bup_ref, wdown_ref,
+    mlp_ref, gn_ref, gup_ref, gdown_ref, gbias_ref,
+    normed_all, normed_tr, cot_all, mlp_acc, gn_acc,
+):
+    step = pl.program_id(0)
+    tok = normed_a.shape[0]
+
+    @pl.when(step == 0)
+    def _():
+        for ref, parts in ((normed_all, (normed_a, normed_b)), (cot_all, (cot_a, cot_b))):
+            ref[:tok, :] = parts[0][...]
+            ref[tok:, :] = parts[1][...]
+        normed_tr[...] = normed_all[...].T
+        mlp_acc[...] = jnp.zeros_like(mlp_acc)
+        gn_acc[...] = jnp.zeros_like(gn_acc)
+
+    w_up, w_down = wup_ref[...], wdown_ref[...]
+    up = dot_nn(normed_all[...], w_up) + bup_ref[...]
+    half_erf = 0.5 * (1.0 + lax.erf(up * SQRT_HALF))
+    activated = (up * half_erf).astype(BF16)
+    slope = half_erf + up * jnp.exp(-0.5 * up * up) * INV_ROOT_TWO_PI
+    grad_up = (dot_nt(cot_all[...], w_down) * slope).astype(BF16)
+    mlp_acc[...] += dot_nn(activated, w_down)
+    gn_acc[...] += dot_nt(grad_up, w_up)
+    gup_ref[...] = dot_nn(normed_tr[...], grad_up).astype(BF16).reshape(gup_ref.shape)
+    gdown_ref[...] = dot_nn(activated.T, cot_all[...]).astype(BF16).reshape(gdown_ref.shape)
+    gbias_ref[...] = jnp.sum(grad_up.astype(F32), axis=0, keepdims=True)
+
+    @pl.when(step == pl.num_programs(0) - 1)
+    def _():
+        mlp_ref[...] = mlp_acc[...].astype(BF16)
+        gn_ref[...] = gn_acc[...].astype(BF16)
+
+
+def feed_forward(normed, normed_peer, cot, cot_peer, w_up, b_up, w_down):
+    tok, width = normed.shape
+    hidden = w_up.shape[1]
+    group = 256
+    steps = hidden // group
+    per = width // group
+    const = lambda shape: pl.BlockSpec(shape, lambda s: (0,) * len(shape))
+    chunks = hidden // CHUNK
+    return pl.pallas_call(
+        feed_forward_kernel,
+        grid=(steps,),
+        out_shape=(
+            jax.ShapeDtypeStruct((2 * tok, width), BF16),
+            jax.ShapeDtypeStruct((2 * tok, width), BF16),
+            jax.ShapeDtypeStruct((chunks, CHUNK, width), BF16),
+            jax.ShapeDtypeStruct((chunks, CHUNK, width), BF16),
+            jax.ShapeDtypeStruct((1, hidden), F32),
+        ),
+        in_specs=[const((tok, width))] * 4
+        + [
+            pl.BlockSpec((width, group), lambda s: (0, s)),
+            pl.BlockSpec((1, group), lambda s: (0, s)),
+            pl.BlockSpec((group, width), lambda s: (s, 0)),
+        ],
+        out_specs=(
+            const((2 * tok, width)),
+            const((2 * tok, width)),
+            pl.BlockSpec((width // CHUNK, CHUNK, group), lambda s: (s // per, 0, s % per)),
+            pl.BlockSpec((group // CHUNK, CHUNK, width), lambda s: (s, 0, 0)),
+            pl.BlockSpec((1, group), lambda s: (0, s)),
+        ),
+        scratch_shapes=[
+            pltpu.VMEM((2 * tok, width), BF16),
+            pltpu.VMEM((width, 2 * tok), BF16),
+            pltpu.VMEM((2 * tok, width), BF16),
+            pltpu.VMEM((2 * tok, width), F32),
+            pltpu.VMEM((2 * tok, width), F32),
+        ],
+        compiler_params=pltpu.CompilerParams(vmem_limit_bytes=VMEM_BIG),
+        name="feed_forward",
+    )(normed, normed_peer, cot, cot_peer, w_up, b_up, w_down)
+
+
+def attention_weights_kernel(
+    normed_a, normed_b, cot_a, cot_b, att_a, att_b, gproj_ref, gproj_peer, small_a, small_b, gbias_ref, out_ref,
+):
+    width = normed_a.shape[1]
+    third = gproj_peer.shape[1]
+    half = width // 2
+    here = lax.axis_index("mlp")
+    group = 512
+    chunks = width // CHUNK
+    normed_tr = jnp.concatenate([normed_a[...], normed_b[...]], axis=0).T
+    for start in range(0, third, group):
+        cols = pl.ds(pl.multiple_of(here * third + start, LANES), group)
+        grads = jnp.concatenate([gproj_ref[:, cols], gproj_peer[:, start : start + group]], axis=0)
+        block, at = start // width, start % width
+        out_ref[block * chunks : (block + 1) * chunks, :, at : at + group] = (
+            dot_nn(normed_tr, grads).astype(BF16).reshape(chunks, CHUNK, group)
+        )
+    cols = pl.ds(pl.multiple_of(here * half, LANES), half)
+    att_tr = jnp.concatenate([att_a[...], att_b[...]], axis=0).T
+    cots = jnp.concatenate([cot_a[:, cols], cot_b[:, cols]], axis=0)
+    out_ref[chunks : 2 * chunks, :, half:] = dot_nn(att_tr, cots).astype(BF16).reshape(chunks, CHUNK, half)
+    rows = small_a[...] + small_b[...]
+    out_ref[2 * chunks] = jnp.concatenate(
+        [rows[:6], gbias_ref[:, :width], gbias_ref[:, width:], jnp.zeros((CHUNK - 8, width), F32)], axis=0
+    ).astype(BF16)
+    out_ref[2 * chunks + 1] = jnp.zeros((CHUNK, width), BF16)
+
+
+def attention_weights(*operands):
+    width = operands[0].shape[1]
+    vmem = pl.BlockSpec(memory_space=pltpu.VMEM)
+    return pl.pallas_call(
+        attention_weights_kernel,
+        out_shape=jax.ShapeDtypeStruct((2 * (width // CHUNK) + 2, CHUNK, width), BF16),
+        in_specs=[vmem] * len(operands),
+        out_specs=vmem,
+        compiler_params=pltpu.CompilerParams(vmem_limit_bytes=VMEM_BIG),
+        name="attention_weights",
+    )(*operands)
+
+
+TREE_PERIOD = 10
+TREE_SPINE = 0b0110101011
+TREE_ROW = (0, 1, 0, 0, 1, 1, 0, 0, 1, 1)
+TREE_ROOT = (1, 2, 0, 2, 3, 1, 2, 1, 2, 1)
+TREE_SPAN = 4
+
+
+def packed_table(values, bits):
+    return sum(v << (bits * i) for i, v in enumerate(values))
+
+
+def tree_roles(i, y, z):
+    kind = lax.rem(i, TREE_PERIOD)
+    bit = lambda table, bits: lax.bitwise_and(
+        lax.shift_right_logical(jnp.int32(table), bits * kind), jnp.int32(2**bits - 1)
+    )
+    spine = bit(TREE_SPINE, 1) == 1
+    row = bit(packed_table(TREE_ROW, 1), 1)
+    root = bit(packed_table(TREE_ROOT, 2), 2)
+    on_row = y == row
+    along = jnp.logical_or(jnp.logical_not(spine), on_row)
+    at_root = z == root
+    left = jnp.logical_and(along, jnp.logical_and(z <= root, z > 0))
+    right = jnp.logical_and(along, jnp.logical_and(z >= root, z < TREE_SPAN - 1))
+    side = jnp.logical_and(on_row, jnp.logical_or(spine, at_root))
+    to_side = jnp.logical_and(jnp.logical_not(on_row), jnp.logical_or(spine, at_root))
+    to_right = jnp.logical_and(along, z < root)
+    to_left = jnp.logical_and(along, z > root)
+    is_root = jnp.logical_and(on_row, at_root)
+    span = jnp.maximum(root, TREE_SPAN - 1 - root)
+    base = jnp.where(spine, 1, 0)
+    height = jnp.where(
+        jnp.logical_and(spine, jnp.logical_not(on_row)), 0,
+        base + jnp.where(z < root, z, jnp.where(z > root, TREE_SPAN - 1 - z, span)),
+    )
+    height = jnp.where(jnp.logical_and(jnp.logical_not(spine), is_root), span + 1, height)
+    top = span + 1
+    depth = top + jnp.abs(z - root) + jnp.where(on_row, 0, 1)
+    return left, right, side, to_left, to_right, to_side, is_root, height, depth
+
+
+def reduce_kernel(lag, counts, *refs):
+    ins, rest = refs[: len(counts)], refs[len(counts) :]
+    out = rest[0]
+    own, sib, from_left, from_right, from_side, acc = rest[1:7]
+    (own_sem, give_sem, sib_recv, up_send, left_recv, right_recv, side_recv, res_recv, pair_recv,
+     keep_sem, down_left, down_right, down_side, down_pair) = rest[7:]
+    total = own.shape[0]
+    me = lax.axis_index("dp")
+    core = lax.rem(me, 2)
+    y = lax.rem(me // 2, 2)
+    z = me // 4
+    pair = me + 1 - 2 * core
+    flip = me + 2 - 4 * y
+    barrier = pltpu.get_barrier_semaphore()
+    go = lambda device: pl.semaphore_signal(barrier, inc=1, device_id={"dp": device}, device_id_type=MESH)
+    go(pair)
+    go(flip)
+
+    @pl.when(z > 0)
+    def _():
+        go(me - 4)
+
+    @pl.when(z < TREE_SPAN - 1)
+    def _():
+        go(me + 4)
+
+    pl.semaphore_wait(barrier, 2 + jnp.where(z > 0, 1, 0) + jnp.where(z < TREE_SPAN - 1, 1, 0))
+
+    remote = lambda src, dst, send, recv, device: pltpu.make_async_remote_copy(
+        src_ref=src, dst_ref=dst, send_sem=send, recv_sem=recv, device_id={"dp": device}, device_id_type=MESH
+    )
+    starts = [sum(counts[:n]) for n in range(len(counts))]
+    give = lambda n, i: remote(ins[n].at[2 * (i - starts[n]) + 1 - core], sib.at[i], give_sem.at[i], sib_recv.at[i], pair)
+    load = lambda n, i: pltpu.make_async_copy(ins[n].at[2 * (i - starts[n]) + core], own.at[i], own_sem.at[i])
+
+    for n, count in enumerate(counts):
+        def begin(i, carry, n=n):
+            give(n, i).start()
+            load(n, i).start()
+            return carry
+
+        lax.fori_loop(starts[n], starts[n] + count, begin, 0)
+
+    up = {
+        "left": lambda i: remote(own.at[i], from_right.at[i], up_send.at[i], right_recv.at[i], me - 4),
+        "right": lambda i: remote(own.at[i], from_left.at[i], up_send.at[i], left_recv.at[i], me + 4),
+        "side": lambda i: remote(own.at[i], from_side.at[i], up_send.at[i], side_recv.at[i], flip),
+    }
+    slot = lambda i: out.at[2 * i + core]
+    down = {
+        "left": lambda src, i: remote(src, slot(i), down_left.at[i], res_recv.at[i], me - 4),
+        "right": lambda src, i: remote(src, slot(i), down_right.at[i], res_recv.at[i], me + 4),
+        "side": lambda src, i: remote(src, slot(i), down_side.at[i], res_recv.at[i], flip),
+        "pair": lambda src, i: remote(src, slot(i), down_pair.at[i], pair_recv.at[i], pair),
+    }
+    keep = lambda i: pltpu.make_async_copy(own.at[i], slot(i), keep_sem.at[i])
+
+    def spread(src, i, left, right, side):
+        for name, there in (("left", left), ("right", right), ("side", side)):
+            @pl.when(there)
+            def _(name=name):
+                down[name](src, i).start()
+
+        down["pair"](src, i).start()
+
+    def ascend(i, roles):
+        left, right, side, to_left, to_right, to_side, is_root, _, _ = roles
+        pltpu.make_async_copy(own.at[i], own.at[i], own_sem.at[i]).wait()
+        remote(own.at[i], sib.at[i], give_sem.at[i], sib_recv.at[i], pair).wait_recv()
+        acc[...] = own[i].astype(F32) + sib[i].astype(F32)
+        for there, land, sem in ((left, from_left, left_recv), (right, from_right, right_recv), (side, from_side, side_recv)):
+            @pl.when(there)
+            def _(land=land, sem=sem):
+                remote(own.at[i], land.at[i], give_sem.at[i], sem.at[i], pair).wait_recv()
+                acc[...] += land[i].astype(F32)
+
+        own[i] = acc[...].astype(BF16)
+        for name, there in (("left", to_left), ("right", to_right), ("side", to_side)):
+            @pl.when(there)
+            def _(name=name):
+                up[name](i).start()
+
+        @pl.when(is_root)
+        def _():
+            keep(i).start()
+            spread(own.at[i], i, left, right, side)
+
+    def descend(i, roles):
+        left, right, side = roles[:3]
+        remote(own.at[i], slot(i), give_sem.at[i], res_recv.at[i], pair).wait_recv()
+        spread(slot(i), i, left, right, side)
+
+    highest, deepest = TREE_SPAN, 2 * TREE_SPAN
+
+    def tick(t, carry):
+        for level in range(highest + 1):
+            i = t - lag * level
+            roles = tree_roles(jnp.maximum(i, 0), y, z)
+
+            @pl.when(jnp.logical_and(jnp.logical_and(i >= 0, i < total), roles[7] == level))
+            def _(i=i, roles=roles):
+                ascend(i, roles)
+
+        for level in range(2, deepest + 1):
+            i = t - lag * level
+            roles = tree_roles(jnp.maximum(i, 0), y, z)
+            here = jnp.logical_and(roles[8] == level, jnp.logical_not(roles[6]))
+
+            @pl.when(jnp.logical_and(jnp.logical_and(i >= 0, i < total), here))
+            def _(i=i, roles=roles):
+                descend(i, roles)
+
+        return carry
+
+    lax.fori_loop(0, total + lag * deepest, tick, 0)
+
+    def drain(i, carry):
+        left, right, side, to_left, to_right, to_side, is_root, _, _ = tree_roles(i, y, z)
+        remote(own.at[i], sib.at[i], give_sem.at[i], sib_recv.at[i], pair).wait_send()
+
+        @pl.when(jnp.logical_not(is_root))
+        def _():
+            up["side"](i).wait_send()
+
+        @pl.when(is_root)
+        def _():
+            keep(i).wait()
+
+        for name, there in (("left", left), ("right", right), ("side", side)):
+            @pl.when(there)
+            def _(name=name):
+                down[name](own.at[i], i).wait_send()
+
+        down["pair"](own.at[i], i).wait_send()
+        remote(own.at[i], out.at[2 * i + 1 - core], give_sem.at[i], pair_recv.at[i], pair).wait_recv()
+        return carry
+
+    lax.fori_loop(0, total, drain, 0)
+
+
+def reduce_chunks(arrays, collective, lag=4):
+    counts = tuple(a.shape[0] // 2 for a in arrays)
+    total = sum(counts)
+    chunk = arrays[0].shape[1:]
+    any_spec = pl.BlockSpec(memory_space=pl.ANY)
+    return pl.pallas_call(
+        functools.partial(reduce_kernel, lag, counts),
+        out_shape=jax.ShapeDtypeStruct((2 * total,) + chunk, BF16),
+        in_specs=[any_spec] * len(arrays),
+        out_specs=any_spec,
+        scratch_shapes=[pltpu.VMEM((total,) + chunk, BF16)] * 5
+        + [pltpu.VMEM(chunk, F32)]
+        + [pltpu.SemaphoreType.DMA((total,))] * 14,
+        compiler_params=pltpu.CompilerParams(
+            collective_id=collective, has_side_effects=True, vmem_limit_bytes=VMEM_BIG
+        ),
+        name="reduce" + str(collective),
+    )(*arrays)
 
 
 def by_heads(
@@ -415,59 +740,40 @@
 
     normed, send = project(x, cot, gain, shift, w_qkv, b_qkv[None], w_out, tables)
     heads, (normed_peer, cot_peer) = exchange(send, (normed, cot), 0)
-
-    normed_all = jnp.concatenate([normed, normed_peer])
-    cot_all = jnp.concatenate([cot, cot_peer])
-    up = dot_nn(normed_all, w_up) + b_up
-    erf_part = 0.5 * (1.0 + lax.erf(up * SQRT_HALF))
-    activated = (up * erf_part).astype(BF16)
-    slope = erf_part + up * jnp.exp(-0.5 * up * up) * INV_ROOT_TWO_PI
-    grad_up = (dot_nt(cot_all, w_down) * slope).astype(BF16)
-    mlp_part = dot_nn(activated, w_down).astype(BF16)
-    gn_part = dot_nt(grad_up, w_up).astype(BF16)
-    grad_w_down = dot_tn(activated, cot_all).astype(BF16)
-    grad_w_up = dot_tn(normed_all, grad_up).astype(BF16)
-    grad_b_up = jnp.sum(grad_up.astype(F32), axis=0).astype(BF16)
-
+    mlp_part, gn_part, sum_up, sum_down, grad_b_up = feed_forward(
+        normed, normed_peer, cot, cot_peer, w_up, b_up[None], w_down
+    )
     done = attention(heads, order)
     back, (mlp_other, gn_other) = exchange(done, (mlp_part[tok:], gn_part[tok:]), 1)
-    output, grad_input, attended, grad_project, small, grad_b_qkv = finish(
+    output, grad_input, attended, grad_project, small = finish(
         back, x, cot, gain, w_qkv, w_out, (b_out + b_down)[None],
         (mlp_part[:tok], mlp_other), (gn_part[:tok], gn_other), tables,
     )
     third = 3 * width // 2
-    gp_here = lax.dynamic_slice_in_dim(grad_project, seq_here * third, third, axis=1)
-    gp_give = lax.dynamic_slice_in_dim(grad_project, (1 - seq_here) * third, third, axis=1)
-    att_peer, gp_peer = swap((attended, gp_give), 2)
-    cot_cols = lax.dynamic_slice_in_dim(cot_all, seq_here * (width // 2), width // 2, axis=1)
-    grad_w_qkv = dot_tn(normed_all, jnp.concatenate([gp_here, gp_peer])).astype(BF16)
-    grad_w_out = dot_tn(jnp.concatenate([attended, att_peer]), cot_cols).astype(BF16)
-
-    everyone = ("dp", "mlp")
-    vec = jnp.concatenate([small[0], small[1], small[2], grad_b_qkv[0]])
-    vec, b_up_sum, s_qkv, s_out, s_up, s_down = (
-        lax.psum(vec, everyone),
-        lax.psum(grad_b_up, "dp"),
-        lax.psum(grad_w_qkv, "dp"),
-        lax.psum(grad_w_out, "dp"),
-        lax.psum(grad_w_up, "dp"),
-        lax.psum(grad_w_down, "dp"),
-    )
     half = width // 2
-    piece = lambda start, size: lax.dynamic_slice_in_dim(vec, start + seq_here * size, size)
-    bias_sum = piece(2 * width, half)
+    give = lax.dynamic_slice_in_dim(grad_project, (1 - seq_here) * third, third, axis=1)
+    att_peer, gproj_peer, small_peer = swap((attended, give, small), 2)
+    sum_att = attention_weights(
+        normed, normed_peer, cot, cot_peer, attended, att_peer, grad_project, gproj_peer, small, small_peer, grad_b_up
+    )
+    summed = reduce_chunks((sum_up, sum_down, sum_att), 3)
+    block = lambda n: summed[n * (width // CHUNK) : (n + 1) * (width // CHUNK)].reshape(width, width).astype(F32)
+    vec = summed[6 * (width // CHUNK), :8].astype(F32)
+    piece = lambda rows, size: lax.dynamic_slice_in_dim(vec[rows].reshape(-1), seq_here * size, size)
+    bias_sum = piece(slice(2, 3), half)
+    last = block(5)
     return (
         output.reshape(1, 1, tok, width),
         grad_input.reshape(1, 1, tok, width),
-        piece(0, half),
-        piece(width, half),
-        s_qkv.astype(F32),
-        piece(3 * width, third),
-        s_out.astype(F32),
+        piece(slice(0, 1), half),
+        piece(slice(1, 2), half),
+        jnp.concatenate([block(4), last[:, :half]], axis=1),
+        piece(slice(3, 6), third),
+        last[:, half:],
         bias_sum,
-        s_up.astype(F32),
-        b_up_sum.astype(F32),
-        s_down.astype(F32),
+        jnp.concatenate([block(0), block(1)], axis=1),
+        vec[6:8].reshape(-1),
+        jnp.concatenate([block(2), block(3)], axis=0),
         bias_sum,
     )
 

time: 453 us -> 354 us (0.78)
  Pallas kernels: 143 us -> 313 us
  waiting for transfers between devices: 158 us -> 0 us
  blocking collectives: 81.1 us -> 0 us
  matrix products: 25.6 us -> 0 us
  between operations: 15 us -> 1.43 us
  local copies, waits for them, and re-layouts: 10.6 us -> 20.5 us
    pallas_call x0 -> x3, Pallas kernels: none -> 169 us  [the longest x1 146 us: reduce_chunks(): pl.pallas_call(functools.partial(reduce_kernel, lag, counts), out_shape=j...]
    psum x1 -> x0, waiting for transfers between devices: 158 us -> none  [by_heads(): lax.psum(grad_w_qkv, 'dp')]
    psum x2 -> x0, blocking collectives: 81.1 us -> none  [the longest x1 48.7 us: by_heads(): lax.psum(vec, everyone)]
    dot_general x8 -> x0, matrix products: 25.6 us -> none  [the longest x4 15.1 us: dot_tn(): lax.dot_general(a, b, (((0,), (0,)), ((), ())), preferred_element_type=F32)]
    convert_element_type x5 -> x3, other arithmetic: 17 us -> 1.9 us  [the longest x2 1.18 us: by_heads(): summed[n * (width // CHUNK):(n + 1) * (width // CHUNK)]]
    concatenate x1 -> x3, other arithmetic: 0.01 us -> 14.5 us  [the longest x1 6.77 us: by_heads(): jnp.concatenate([block(0), block(1)], axis=1)]
    slice x1 -> x4, local copies, waits for them, and re-layouts: 0.88 us -> 9.71 us  [the longest x1 7.91 us: by_heads(): summed[n * (width // CHUNK):(n + 1) * (width // CHUNK)]]
  transfers between devices with their start and end apart: 1 -> 0, of which waited for: 1 -> 0; matrix products, arithmetic and copies ran while one was open for 1% -> 0% of each run, Pallas kernels for 0% -> 0%
where the time goes in v2:
time: 354 us; the launch traced here: 353 us
  Pallas kernels  313 us (88%)
  local copies, waits for them, and re-layouts  20.5 us (6%)
  other arithmetic  18.8 us (5%)
    pallas_call x1, Pallas kernels, reduce_chunks(): pl.pallas_call(functools.partial(reduce_kernel, lag, counts), out_shape=j...  146 us
    pallas_call x2, Pallas kernels, exchange(): pl.pallas_call(functools.partial(exchange_kernel, count, peers, None), ou...  61.3 us
    pallas_call x1, Pallas kernels, attention(): pl.pallas_call(functools.partial(attention_kernel, tile), out_shape=jax.S...  45.2 us
    pallas_call x1, Pallas kernels, swap(): pl.pallas_call(functools.partial(swap_kernel, count), out_shape=tuple((ja...  20.8 us
    pallas_call x1, Pallas kernels, feed_forward(): pl.pallas_call(feed_forward_kernel, grid=(steps,), out_shape=(jax.ShapeDt...  16.8 us
    pallas_call x1, Pallas kernels, finish(): pl.pallas_call(finish_kernel, out_shape=(jax.ShapeDtypeStruct((tok, width...  8.95 us
    slice x1, local copies, waits for them, and re-layouts, by_heads(): summed[n * (width // CHUNK):(n + 1) * (width // CHUNK)]  7.91 us
    pallas_call x1, Pallas kernels, project(): pl.pallas_call(project_kernel, grid=(steps,), out_shape=(jax.ShapeDtypeSt...  7.1 us

profile of v2, /device:TPU:0, one launch (start us, length us, event | category | flops | bytes accessed | tf_op | source)
XLA Modules:
  0.0 353.4 jit_solution(5003471160800114515)
XLA Ops:
  0.6 0.7 fusion.4
  1.3 0.6 select_reduce_fusion.order_ref
  2.0 1.3 dynamic_slice.30
  3.9 0.4 fusion.3
  4.3 0.7 pad_maximum_fusion.1.tab_ref
  5.0 7.1 %project.1 = (bf16[160,1024]{1,0:T(8,128)(2,1)}, bf16[16,160,256]{2,1,0:T(8,128)(2,1)}) custom-call(bf16[160,1024]{1,0:T(8,128)(2,1)} %bitcast.39, bf16[160,1024]{1,0:T(8,128)(2,1)} %bitcast.34, f32[1,1024]{1,0:T(1,128)} %bitcast.44, f32[1,1024]{1,0:T(1,128)} %bitcast.51, bf16[1024,3072]{1,0:T(8,128)(2,1)} %wqkv_ref.1, bf16[1024,3072]{1,0:T(8,128)(2,1)} %wqkv_ref.1, ...), custom_call_target="tpu_custom_call" | custom-call | tf_op jit(solution)/shard_map/project/pallas_call | solution.py:105
  12.1 28.3 %exchange0.1 = (bf16[16,160,256]{2,1,0:T(8,128)(2,1)}, bf16[160,1024]{1,0:T(8,128)(2,1)}, bf16[160,1024]{1,0:T(8,128)(2,1)}) custom-call(bf16[16,160,256]{2,1,0:T(8,128)(2,1)} %get-tuple-element.33.refs_0_, bf16[160,1024]{1,0:T(8,128)(2,1)} %get-tuple-element.34.refs_1_.normed_a, bf16[160,1024]{1,0:T(8,128)(2,1)} %bitcast.35), custom_call_target="tpu_custom_call" | custom-call | tf_op jit(solution)/shard_map/exchange0/pallas_call | solution.py:170
  40.4 45.2 %attention.1.refs_0_ = bf16[16,160,256]{2,1,0:T(8,128)(2,1)} custom-call(s32[16]{0:T(128)} %select_reduce_fusion.order_ref, bf16[16,160,256]{2,1,0:T(8,128)(2,1)} %get-tuple-element.35.in_ref), custom_call_target="tpu_custom_call" | custom-call | tf_op jit(solution)/shard_map/attention/pallas_call | solution.py:322
  85.7 16.8 %feed_forward.1 = (bf16[320,1024]{1,0:T(8,128)(2,1)}, bf16[320,1024]{1,0:T(8,128)(2,1)}, bf16[32,64,1024]{2,1,0:T(8,128)(2,1)}, bf16[32,64,1024]{2,1,0:T(8,128)(2,1)}, f32[1,2048]{1,0:T(1,128)}) custom-call(bf16[160,1024]{1,0:T(8,128)(2,1)} %get-tuple-element.34.refs_1_.normed_a, bf16[160,1024]{1,0:T(8,128)(2,1)} %get-tuple-element.36.normed_b, ...), custom_call_target="tpu_custom_call" | custom-call | tf_op jit(solution)/shard_map/feed_forward/pallas_call | solution.py:449
  102.4 0.0 copy-start.2
  102.4 2.0 fusion.13
  104.4 1.9 fusion.12
  106.3 33.0 %exchange1.1 = (bf16[16,160,256]{2,1,0:T(8,128)(2,1)}, bf16[160,1024]{1,0:T(8,128)(2,1)}, bf16[160,1024]{1,0:T(8,128)(2,1)}) custom-call(bf16[16,160,256]{2,1,0:T(8,128)(2,1)} %attention.1.refs_0_, bf16[160,1024]{1,0:T(8,128)(2,1)} %get-tuple-element.65.refs_1_, bf16[160,1024]{1,0:T(8,128)(2,1)} %get-tuple-element.63.refs_2_), custom_call_target="tpu_custom_call" | custom-call | tf_op jit(solution)/shard_map/exchange1/pallas_call | solution.py:170
  139.4 0.6 add.64
  140.0 8.9 %finish.1 = (bf16[160,1024]{1,0:T(8,128)(2,1)}, f32[160,1024]{1,0:T(8,128)}, bf16[160,1024]{1,0:T(8,128)(2,1)}, bf16[160,3072]{1,0:T(8,128)(2,1)}, f32[8,1024]{1,0:T(8,128)}) custom-call(bf16[16,160,256]{2,1,0:T(8,128)(2,1)} %get-tuple-element.40.heads_ref, bf16[160,1024]{1,0:T(8,128)(2,1)} %bitcast.40, bf16[160,1024]{1,0:T(8,128)(2,1)} %bitcast.37, ...), custom_call_target="tpu_custom_call" | custom-call | tf_op jit(solution)/shard_map/finish/pallas_call | solution.py:387
  148.9 1.8 constant_dynamic-slice_fusion.2.refs_1_
  150.7 20.8 %swap2.1 = (bf16[160,1024]{1,0:T(8,128)(2,1)}, bf16[160,1536]{1,0:T(8,128)(2,1)}, f32[8,1024]{1,0:T(8,128)}) custom-call(bf16[160,1024]{1,0:T(8,128)(2,1)} %get-tuple-element.47.refs_0_.att_a, bf16[160,1536]{1,0:T(8,128)(2,1)} %constant_dynamic-slice_fusion.2.refs_1_, f32[8,1024]{1,0:T(8,128)} %get-tuple-element.49.refs_2_.small_a), custom_call_target="tpu_custom_call" | custom-call | tf_op jit(solution)/shard_map/swap2/pallas_call | solution.py:212
  171.5 6.5 %attention_weights.1.refs_2_ = bf16[34,64,1024]{2,1,0:T(8,128)(2,1)} custom-call(bf16[160,1024]{1,0:T(8,128)(2,1)} %get-tuple-element.34.refs_1_.normed_a, bf16[160,1024]{1,0:T(8,128)(2,1)} %get-tuple-element.36.normed_b, bf16[160,1024]{1,0:T(8,128)(2,1)} %bitcast.38, bf16[160,1024]{1,0:T(8,128)(2,1)} %get-tuple-element.37.cot_b, ...), custom_call_target="tpu_custom_call" | custom-call | tf_op jit(solution)/shard_map/attention_weights/pallas_call | solution.py:515
  178.0 146.2 %reduce3.1 = bf16[98,64,1024]{2,1,0:T(8,128)(2,1)} custom-call(bf16[32,64,1024]{2,1,0:T(8,128)(2,1)} %get-tuple-element.45.refs_0_, bf16[32,64,1024]{2,1,0:T(8,128)(2,1)} %get-tuple-element.46.refs_1_, bf16[34,64,1024]{2,1,0:T(8,128)(2,1)} %attention_weights.1.refs_2_), custom_call_target="tpu_custom_call" | custom-call | tf_op jit(solution)/shard_map/reduce3/pallas_call | solution.py:711
  324.2 0.7 slice_convert_fusion
  324.9 0.6 constant_dynamic-slice_fusion.1
  325.5 0.6 constant_dynamic-slice_fusion
  326.1 7.9 %fusion.10 = (bf16[16,64,1024]{2,1,0:T(8,128)(2,1)S(1)}, bf16[16,64,1024]{2,1,0:T(8,128)(2,1)}, bf16[16,64,1024]{2,1,0:T(8,128)(2,1)}, bf16[16,64,1024]{2,1,0:T(...) fusion(bf16[98,64,1024]{2,1,0:T(8,128)(2,1)} %reduce3.1), kind=kLoop, calls=%fused_computation.36 | loop fusion | bytes 25165824 | tf_op jit(solution)/shard_map/slice | solution.py:760
  334.0 0.6 bitcast_convert_fusion.1
  334.6 1.8 fusion.11
  336.4 0.6 bitcast_convert_fusion
  337.0 3.3 pad_maximum_fusion
  340.3 0.7 dynamic_slice.36
  341.0 6.8 %maximum_convert_fusion = f32[1024,2048]{1,0:T(8,128)} fusion(bf16[1024,1024]{1,0:T(8,128)(2,1)} %bitcast.32, bf16[1024,1024]{1,0:T(8,128)(2,1)} %bitcast.33), kind=kLoop, calls=%fused_computation.1 | loop fusion | flops 8388608 | bytes 12582912 | tf_op jit(solution)/shard_map/concatenate | solution.py:774
  347.7 0.6 copy.27
  348.3 4.5 %maximum_convert_fusion.1 = f32[2048,1024]{1,0:T(8,128)} fusion(bf16[1024,1024]{1,0:T(8,128)(2,1)S(1)} %bitcast.31, bf16[1024,1024]{1,0:T(8,128)(2,1)S(1)} %bitcast.30), kind=kLoop, calls=%fused_computation.2 | loop fusion | flops 8388608 | bytes 12582912 | tf_op jit(solution)/shard_map/concatenate | solution.py:776
  352.8 0.6 copy.29
  (16 shorter events, 0.1 us)
Async XLA Ops:
  102.4 36.9 %copy-start.2 = (f32[1024]{0:T(1024)S(1)}, f32[1024]{0:T(1024)}, u32[]{:S(2)}) copy-start(f32[1024]{0:T(1024)} %param.20) | copy-start | bytes 12292
  102.4 36.9 %copy-start.3 = (f32[1024]{0:T(1024)S(1)}, f32[1024]{0:T(1024)}, u32[]{:S(2)}) copy-start(f32[1024]{0:T(1024)} %param.24) | copy-start | bytes 12292
  341.0 11.9 %copy-start.1 = (f32[1,1,512]{2,1,0:T(1,128)}, f32[1,1,512]{2,1,0:T(1,128)S(1)}, u32[]{:S(2)}) copy-start(f32[1,1,512]{2,1,0:T(1,128)S(1)} %constant_dynamic-slice_fusion.3) | copy-start | bytes 6148
  341.0 7.4 %copy-start = (bf16[16,64,1024]{2,1,0:T(8,128)(2,1)S(1)}, bf16[16,64,1024]{2,1,0:T(8,128)(2,1)}, u32[]{:S(2)}) copy-start(bf16[16,64,1024]{2,1,0:T(8,128)(2,1)} %get-tuple-element.55) | copy-start | bytes 6291460

commit v3 on v1

--- a/solution.py
+++ b/solution.py
@@ -22,6 +22,10 @@
 BF16 = jnp.bfloat16
 LANES = 128
 VMEM_BIG = 60 * 1024 * 1024
+TREE_LAG = 4
+TREE_GAP = 12
+TICKS_PER_BLOCK = 2
+VMEM_ALL = 66 * 1024 * 1024 - 2**20 // 2
 
 
 def dot_nn(a, b):
@@ -186,42 +190,314 @@
     return out[0], out[1:]
 
 
-def swap_kernel(count, *refs):
-    ins, outs = refs[:count], refs[count : 2 * count]
-    send, recv = refs[2 * count :]
-    other = 1 - lax.axis_index("mlp")
-    barrier = pltpu.get_barrier_semaphore()
-    pl.semaphore_signal(barrier, inc=1, device_id={"mlp": other}, device_id_type=MESH)
-    pl.semaphore_wait(barrier, 1)
-    copies = [
-        pltpu.make_async_remote_copy(
-            src_ref=ins[i], dst_ref=outs[i], send_sem=send.at[i], recv_sem=recv.at[i],
-            device_id={"mlp": other}, device_id_type=MESH,
+CHUNK = 64
+
+
+def feed_forward_kernel(
+    normed_a, normed_b, cot_a, cot_b, wup_ref, bup_ref, wdown_ref,
+    mlp_ref, mlp_give, gn_ref, gn_give, gup_ref, gdown_ref, gbias_ref,
+    normed_all, normed_tr, cot_all, mlp_acc, gn_acc,
+):
+    step = pl.program_id(0)
+    tok = normed_a.shape[0]
+
+    @pl.when(step == 0)
+    def _():
+        for ref, parts in ((normed_all, (normed_a, normed_b)), (cot_all, (cot_a, cot_b))):
+            ref[:tok, :] = parts[0][...]
+            ref[tok:, :] = parts[1][...]
+        normed_tr[...] = normed_all[...].T
+        mlp_acc[...] = jnp.zeros_like(mlp_acc)
+        gn_acc[...] = jnp.zeros_like(gn_acc)
+
+    w_up, w_down = wup_ref[...], wdown_ref[...]
+    up = dot_nn(normed_all[...], w_up) + bup_ref[...]
+    half_erf = 0.5 * (1.0 + lax.erf(up * SQRT_HALF))
+    activated = (up * half_erf).astype(BF16)
+    slope = half_erf + up * jnp.exp(-0.5 * up * up) * INV_ROOT_TWO_PI
+    grad_up = (dot_nt(cot_all[...], w_down) * slope).astype(BF16)
+    mlp_acc[...] += dot_nn(activated, w_down)
+    gn_acc[...] += dot_nt(grad_up, w_up)
+    gup_ref[...] = dot_nn(normed_tr[...], grad_up).astype(BF16).reshape(gup_ref.shape)
+    gdown_ref[...] = dot_nn(activated.T, cot_all[...]).astype(BF16).reshape(gdown_ref.shape)
+    gbias_ref[...] = jnp.sum(grad_up.astype(F32), axis=0, keepdims=True)
+
+    @pl.when(step == pl.num_programs(0) - 1)
+    def _():
+        mlp_ref[...] = mlp_acc[:tok, :].astype(BF16)
+        mlp_give[...] = mlp_acc[tok:, :].astype(BF16)
+        gn_ref[...] = gn_acc[:tok, :].astype(BF16)
+        gn_give[...] = gn_acc[tok:, :].astype(BF16)
+
+
+def feed_forward(normed, normed_peer, cot, cot_peer, w_up, b_up, w_down):
+    tok, width = normed.shape
+    hidden = w_up.shape[1]
+    group = 256
+    steps = hidden // group
+    per = width // group
+    const = lambda shape: pl.BlockSpec(shape, lambda s: (0,) * len(shape))
+    chunks = hidden // CHUNK
+    return pl.pallas_call(
+        feed_forward_kernel,
+        grid=(steps,),
+        out_shape=(jax.ShapeDtypeStruct((tok, width), BF16),) * 4
+        + (
+            jax.ShapeDtypeStruct((chunks, CHUNK, width), BF16),
+            jax.ShapeDtypeStruct((chunks, CHUNK, width), BF16),
+            jax.ShapeDtypeStruct((1, hidden), F32),
+        ),
+        in_specs=[const((tok, width))] * 4
+        + [
+            pl.BlockSpec((width, group), lambda s: (0, s)),
+            pl.BlockSpec((1, group), lambda s: (0, s)),
+            pl.BlockSpec((group, width), lambda s: (s, 0)),
+        ],
+        out_specs=(const((tok, width)),) * 4
+        + (
+            pl.BlockSpec((width // CHUNK, CHUNK, group), lambda s: (s // per, 0, s % per)),
+            pl.BlockSpec((group // CHUNK, CHUNK, width), lambda s: (s, 0, 0)),
+            pl.BlockSpec((1, group), lambda s: (0, s)),
+        ),
+        scratch_shapes=[
+            pltpu.VMEM((2 * tok, width), BF16),
+            pltpu.VMEM((width, 2 * tok), BF16),
+            pltpu.VMEM((2 * tok, width), BF16),
+            pltpu.VMEM((2 * tok, width), F32),
+            pltpu.VMEM((2 * tok, width), F32),
+        ],
+        compiler_params=pltpu.CompilerParams(vmem_limit_bytes=VMEM_BIG),
+        name="feed_forward",
+    )(normed, normed_peer, cot, cot_peer, w_up, b_up, w_down)
+
+
+TREE_PERIOD = 10
+TREE_SPINE = 0b0110101011
+TREE_ROW = (0, 1, 0, 0, 1, 1, 0, 0, 1, 1)
+TREE_ROOT = (1, 2, 0, 2, 3, 1, 2, 1, 2, 1)
+TREE_SPAN = 4
+
+
+def packed_table(values, bits):
+    return sum(v << (bits * i) for i, v in enumerate(values))
+
+
+def tree_roles(i, y, z):
+    kind = lax.rem(i, TREE_PERIOD)
+    bit = lambda table, bits: lax.bitwise_and(
+        lax.shift_right_logical(jnp.int32(table), bits * kind), jnp.int32(2**bits - 1)
+    )
+    spine = bit(TREE_SPINE, 1) == 1
+    row = bit(packed_table(TREE_ROW, 1), 1)
+    root = bit(packed_table(TREE_ROOT, 2), 2)
+    on_row = y == row
+    along = jnp.logical_or(jnp.logical_not(spine), on_row)
+    at_root = z == root
+    left = jnp.logical_and(along, jnp.logical_and(z <= root, z > 0))
+    right = jnp.logical_and(along, jnp.logical_and(z >= root, z < TREE_SPAN - 1))
+    side = jnp.logical_and(on_row, jnp.logical_or(spine, at_root))
+    to_side = jnp.logical_and(jnp.logical_not(on_row), jnp.logical_or(spine, at_root))
+    to_right = jnp.logical_and(along, z < root)
+    to_left = jnp.logical_and(along, z > root)
+    is_root = jnp.logical_and(on_row, at_root)
+    span = jnp.maximum(root, TREE_SPAN - 1 - root)
+    base = jnp.where(spine, 1, 0)
+    height = jnp.where(
+        jnp.logical_and(spine, jnp.logical_not(on_row)), 0,
+        base + jnp.where(z < root, z, jnp.where(z > root, TREE_SPAN - 1 - z, span)),
+    )
+    height = jnp.where(jnp.logical_and(jnp.logical_not(spine), is_root), span + 1, height)
+    top = span + 1
+    depth = top + jnp.abs(z - root) + jnp.where(on_row, 0, 1)
+    flags = (left, right, side, to_left, to_right, to_side, is_root)
+    packed = sum(jnp.where(flag, 1 << n, 0) for n, flag in enumerate(flags))
+    return packed + height * 128 + jnp.where(is_root, 0, depth) * 2048
+
+
+def has(roles, n):
+    return lax.bitwise_and(roles, jnp.int32(1 << n)) != 0
+
+
+class Reducer:
+    def __init__(self, sources, out, buffers, semaphores, lag, early, gap):
+        self.sources, self.out, self.lag, self.early, self.gap = sources, out, lag, early, gap
+        self.own, self.sib, self.lands, self.acc = buffers[0], buffers[1], buffers[2:5], buffers[5]
+        (self.own_sem, self.give_sem, self.sib_recv, self.up_send) = semaphores[:4]
+        self.land_recv = semaphores[4:7]
+        self.res_recv, self.pair_recv, self.keep_sem = semaphores[7:10]
+        self.down_send = semaphores[10:13]
+        self.down_pair = semaphores[13]
+        self.total = self.own.shape[0]
+        self.ticks = self.total + gap + 2 * TREE_SPAN * lag
+        me = lax.axis_index("dp")
+        self.core = lax.rem(me, 2)
+        self.y = lax.rem(me // 2, 2)
+        self.z = me // 4
+        self.pair = me + 1 - 2 * self.core
+        self.near = (me - 4, me + 4, me + 2 - 4 * self.y)
+
+    def remote(self, src, dst, send, recv, device):
+        return pltpu.make_async_remote_copy(
+            src_ref=src, dst_ref=dst, send_sem=send, recv_sem=recv, device_id={"dp": device}, device_id_type=MESH
         )
-        for i in range(count)
-    ]
-    for copy in copies:
-        copy.start()
-    for copy in copies:
-        copy.wait()
-
-
-def swap(arrays, collective):
-    count = len(arrays)
-    any_spec = pl.BlockSpec(memory_space=pl.ANY)
-    return pl.pallas_call(
-        functools.partial(swap_kernel, count),
-        out_shape=tuple(jax.ShapeDtypeStruct(a.shape, a.dtype) for a in arrays),
-        in_specs=[any_spec] * count,
-        out_specs=(any_spec,) * count,
-        scratch_shapes=[pltpu.SemaphoreType.DMA((count,)), pltpu.SemaphoreType.DMA((count,))],
-        compiler_params=pltpu.CompilerParams(collective_id=collective, has_side_effects=True),
-        name="swap" + str(collective),
-    )(*arrays)
+
+    def arrival(self, dst, recv, i):
+        return self.remote(self.own.at[i], dst, self.give_sem.at[i], recv.at[i], self.pair)
+
+    def slot(self, i):
+        return self.out.at[2 * i + self.core]
+
+    def begin(self, which=None):
+        start = 0
+        for n, (ref, offset, count) in enumerate(self.sources):
+            if which is None or n in which:
+                def body(i, carry, ref=ref, offset=offset, start=start):
+                    at = 2 * (i - start + offset)
+                    self.remote(
+                        ref.at[at + 1 - self.core], self.sib.at[i], self.give_sem.at[i], self.sib_recv.at[i], self.pair
+                    ).start()
+                    pltpu.make_async_copy(ref.at[at + self.core], self.own.at[i], self.own_sem.at[i]).start()
+                    return carry
+
+                lax.fori_loop(start, start + count, body, 0)
+            start += count
+
+    def up(self, n, i):
+        other = (1, 0, 2)[n]
+        return self.remote(self.own.at[i], self.lands[other].at[i], self.up_send.at[i], self.land_recv[other].at[i], self.near[n])
+
+    def down(self, n, src, i):
+        return self.remote(src, self.slot(i), self.down_send[n].at[i], self.res_recv.at[i], self.near[n])
+
+    def share(self, src, i):
+        return self.remote(src, self.slot(i), self.down_pair.at[i], self.pair_recv.at[i], self.pair)
+
+    def keep(self, i):
+        return pltpu.make_async_copy(self.own.at[i], self.slot(i), self.keep_sem.at[i])
+
+    def spread(self, src, i, roles):
+        for n in range(3):
+            @pl.when(has(roles, n))
+            def _(n=n):
+                self.down(n, src, i).start()
+
+        self.share(src, i).start()
+
+    def ascend(self, i, roles):
+        own, sib, acc = self.own, self.sib, self.acc
+        pltpu.make_async_copy(own.at[i], own.at[i], self.own_sem.at[i]).wait()
+        self.arrival(sib.at[i], self.sib_recv, i).wait_recv()
+        leaf = lax.bitwise_and(roles, jnp.int32(7)) == 0
+
+        @pl.when(leaf)
+        def _():
+            own[i] = (own[i].astype(F32) + sib[i].astype(F32)).astype(BF16)
+
+        @pl.when(jnp.logical_not(leaf))
+        def _():
+            acc[...] = own[i].astype(F32) + sib[i].astype(F32)
+            for n in range(3):
+                @pl.when(has(roles, n))
+                def _(n=n):
+                    self.arrival(self.lands[n].at[i], self.land_recv[n], i).wait_recv()
+                    acc[...] += self.lands[n][i].astype(F32)
+
+            own[i] = acc[...].astype(BF16)
+
+        for n in range(3):
+            @pl.when(has(roles, 3 + n))
+            def _(n=n):
+                self.up(n, i).start()
+
+        @pl.when(has(roles, 6))
+        def _():
+            self.keep(i).start()
+            self.spread(own.at[i], i, roles)
+
+    def descend(self, i, roles):
+        self.arrival(self.slot(i), self.res_recv, i).wait_recv()
+        self.spread(self.slot(i), i, roles)
+
+    def tick(self, t):
+        for level in range(2 * TREE_SPAN + 1):
+            at = t - self.lag * level
+            late = at >= self.early
+            i = at - jnp.where(late, self.gap, 0)
+            inside = jnp.logical_and(at >= 0, i < self.total)
+            inside = jnp.logical_and(inside, jnp.logical_or(jnp.logical_not(late), i >= self.early))
+            roles = tree_roles(jnp.clip(i, 0, self.total - 1), self.y, self.z)
+            if level <= TREE_SPAN:
+                @pl.when(jnp.logical_and(inside, lax.bitwise_and(roles, jnp.int32(15 * 128)) == level * 128))
+                def _(i=i, roles=roles):
+                    self.ascend(i, roles)
+
+            if level >= 2:
+                @pl.when(jnp.logical_and(inside, lax.bitwise_and(roles, jnp.int32(15 * 2048)) == level * 2048))
+                def _(i=i, roles=roles):
+                    self.descend(i, roles)
+
+    def run(self, first, last):
+        def body(t, carry):
+            self.tick(t)
+            return carry
+
+        lax.fori_loop(first, last, body, 0)
+
+    def drain(self):
+        own = self.own
+
+        def body(i, carry):
+            roles = tree_roles(i, self.y, self.z)
+            self.remote(own.at[i], self.sib.at[i], self.give_sem.at[i], self.sib_recv.at[i], self.pair).wait_send()
+
+            @pl.when(jnp.logical_not(has(roles, 6)))
+            def _():
+                self.up(2, i).wait_send()
+
+            @pl.when(has(roles, 6))
+            def _():
+                self.keep(i).wait()
+
+            for n in range(3):
+                @pl.when(has(roles, n))
+                def _(n=n):
+                    self.down(n, own.at[i], i).wait_send()
+
+            self.share(own.at[i], i).wait_send()
+            self.arrival(self.out.at[2 * i + 1 - self.core], self.pair_recv, i).wait_recv()
+            return carry
+
+        lax.fori_loop(0, self.total, body, 0)
+
+
+def reducer_scratch(total, chunk):
+    return (
+        [pltpu.VMEM((total,) + chunk, BF16)] * 5
+        + [pltpu.VMEM(chunk, F32)]
+        + [pltpu.SemaphoreType.DMA((total,))] * 14
+    )
+
+
+REDUCER_BUFFERS, REDUCER_REFS = 6, 20
+
+
+def greet(barrier, peers):
+    me = lax.axis_index("dp")
+    for step in range(1, peers):
+        pl.semaphore_signal(barrier, inc=1, device_id={"dp": lax.rem(me + step, peers)}, device_id_type=MESH)
+    pl.semaphore_signal(barrier, inc=1, device_id={"mlp": 1 - lax.axis_index("mlp")}, device_id_type=MESH)
+    pl.semaphore_wait(barrier, peers)
+
+
+def to_peer(src, dst, send, recv):
+    return pltpu.make_async_remote_copy(
+        src_ref=src, dst_ref=dst, send_sem=send, recv_sem=recv,
+        device_id={"mlp": 1 - lax.axis_index("mlp")}, device_id_type=MESH,
+    )
 
 
 def attention_kernel(
-    tile, order_ref, in_ref, out_ref,
+    tile, order_ref, place_ref, in_ref, angle_ref, stage,
     q_nat, k_nat, v_nat, k_tr, v_tr, g_tr, probs, kv_grad, aq_out,
 ):
     spans, tok, _ = in_ref.shape
@@ -237,18 +513,10 @@
         q_nat[rows, :] = jnp.concatenate([data[:, :HEAD_DIM] * jnp.asarray(scale, BF16), zeros], axis=1)
         k_nat[rows, :] = data[:, HEAD_DIM : 2 * HEAD_DIM]
         v_nat[rows, :] = data[:, 2 * HEAD_DIM : 3 * HEAD_DIM]
+        aq_out[rows, :HEAD_DIM] = data[:, 3 * HEAD_DIM :]
         return carry
 
     lax.fori_loop(0, spans, gather, 0)
-
-    def gather_grad(place, carry):
-        span = order_ref[place]
-        rows = pl.ds(pl.multiple_of(place * tok, tok), tok)
-        g_nat_rows = in_ref[span][:, 3 * HEAD_DIM :]
-        aq_out[rows, :HEAD_DIM] = g_nat_rows
-        return carry
-
-    lax.fori_loop(0, spans, gather_grad, 0)
 
     def flip(block, carry):
         rows = pl.ds(pl.multiple_of(block * tile, tile), tile)
@@ -264,6 +532,12 @@
     query_col = lax.broadcasted_iota(jnp.int32, (tile, tile), 1)
     causal = key_row <= query_col
     pad = jnp.zeros((tile, HEAD_DIM), BF16)
+    half_rot = ROT // 2
+
+    def turn_back(grad, rows):
+        cosine, sine = angle_ref[0, :, rows], angle_ref[1, :, rows]
+        first, second = grad[:half_rot], grad[half_rot:ROT]
+        return jnp.concatenate([first * cosine + second * sine, second * cosine - first * sine, grad[ROT:]], axis=0)
 
     def query_block(block, carry):
         q_rows = pl.ds(pl.multiple_of(block * tile, tile), tile)
@@ -299,30 +573,41 @@
             return grad_q + dot_nn(k_tr[:, rows], grad_scores)
 
         grad_q = lax.fori_loop(0, block + 1, backward, jnp.zeros((HEAD_DIM, tile), F32))
-        aq_out[q_rows, :] = jnp.concatenate([attended, grad_q * scale], axis=0).T.astype(BF16)
+        aq_out[q_rows, :] = jnp.concatenate([attended, turn_back(grad_q * scale, q_rows)], axis=0).T.astype(BF16)
         return carry
 
     lax.fori_loop(0, blocks, query_block, 0)
 
-    def scatter(place, carry):
-        span = order_ref[place]
-        rows = pl.ds(pl.multiple_of(place * tok, tok), tok)
-        out_ref[span, :, : 2 * HEAD_DIM] = aq_out[rows, :]
-        out_ref[span, :, 2 * HEAD_DIM :] = kv_grad[rows, :].astype(BF16)
+    def turn_keys(block, carry):
+        rows = pl.ds(pl.multiple_of(block * tile, tile), tile)
+        kv_grad[rows, :] = turn_back(kv_grad[rows, :].T, rows).T
         return carry
 
-    lax.fori_loop(0, spans, scatter, 0)
-
-
-def attention(heads, order):
+    lax.fori_loop(0, blocks, turn_keys, 0)
+
+    def fill(span, carry):
+        rows = pl.ds(pl.multiple_of(place_ref[span] * tok, tok), tok)
+        stage[span, :, : 2 * HEAD_DIM] = aq_out[rows, :]
+        stage[span, :, 2 * HEAD_DIM :] = kv_grad[rows, :].astype(BF16)
+        return carry
+
+    lax.fori_loop(0, spans, fill, 0)
+
+
+def attention(heads, order, places):
     spans, tok, width = heads.shape
     length = spans * tok
     tile = 256
+    half_rot = ROT // 2
+    frequency = ROPE_BASE ** (-(jnp.arange(half_rot, dtype=F32) * 2.0 / ROT))
+    angles = frequency[:, None] * jnp.arange(length, dtype=F32)[None, :]
+    angle_tables = jnp.stack([jnp.cos(angles), jnp.sin(angles)])
     vmem = pl.BlockSpec(memory_space=pltpu.VMEM)
+    smem = pl.BlockSpec(memory_space=pltpu.SMEM)
     return pl.pallas_call(
         functools.partial(attention_kernel, tile),
         out_shape=jax.ShapeDtypeStruct(heads.shape, BF16),
-        in_specs=[pl.BlockSpec(memory_space=pltpu.SMEM), vmem],
+        in_specs=[smem, smem, vmem, vmem],
         out_specs=vmem,
         scratch_shapes=[
             pltpu.VMEM((length, 2 * HEAD_DIM), BF16),
@@ -336,32 +621,107 @@
             pltpu.VMEM((length, 2 * HEAD_DIM), BF16),
         ],
         compiler_params=pltpu.CompilerParams(vmem_limit_bytes=VMEM_BIG),
+        cost_estimate=pl.CostEstimate(flops=40 * 10**9, bytes_accessed=10**7, transcendentals=10**7),
         name="attention",
-    )(order, heads)
-
-
-def finish_kernel(
-    heads_ref, x_ref, cot_ref, gain_ref, wqkv_ref, wout_ref, bias_ref, mlp_a, mlp_b, gn_a, gn_b, tab_ref,
-    out_ref, grad_in_ref, att_ref, gproj_ref, small_ref, bqkv_ref,
+    )(order, places, heads, angle_tables)
+
+
+def last_kernel(
+    lag, gap, per_block,
+    stage, mlp_in, gn_in, up_in, down_in, wqkv_hbm, wout_hbm,
+    x_ref, cot_ref, cot_peer, normed_ref, normed_peer, gain_ref, bias_ref, mlp_own, gn_own, gbias_ref,
+    out_ref, grad_in_ref, summed, *scratch,
 ):
+    (heads_own, heads_peer, mlp_other, gn_other, wqkv_ref, wout_ref, att_ref, att_peer, gproj_ref, gproj_peer, normed_tr,
+     sums_ref, small_ref, landing) = scratch[:14]
+    (head_send, head_recv, relay_send, relay_recv, pair_send, pair_recv, local_sem, load_sem, swap_send, swap_recv) = scratch[14:24]
+    buffers = scratch[24:]
+    spans = stage.shape[0]
     tok, width = x_ref.shape
-    tables = [tab_ref[i] for i in range(3)]
+    chunks = width // CHUNK
+    me = lax.axis_index("dp")
+    here = lax.axis_index("mlp")
+    greet(pltpu.get_barrier_semaphore(), spans)
+    pairs = [
+        to_peer(src, dst, pair_send.at[n], pair_recv.at[n])
+        for n, (src, dst) in enumerate(((mlp_in, mlp_other), (gn_in, gn_other)))
+    ]
+    loads = [
+        pltpu.make_async_copy(src, dst, load_sem.at[n])
+        for n, (src, dst) in enumerate(((wqkv_hbm, wqkv_ref), (wout_hbm, wout_ref)))
+    ]
+
+    def block_copy(step):
+        target = lax.rem(me + step, spans)
+        return pltpu.make_async_remote_copy(
+            src_ref=stage.at[target], dst_ref=heads_own.at[me], send_sem=head_send.at[step], recv_sem=head_recv.at[step],
+            device_id={"dp": target}, device_id_type=MESH,
+        )
+
+    def relay(source_ref, step):
+        source = lax.rem(me + spans - step, spans)
+        return to_peer(source_ref.at[source], heads_peer.at[source], relay_send.at[step], relay_recv.at[step])
+
+    for step in range(1, spans):
+        block_copy(step).start()
+    relay(stage, 0).start()
+    own = pltpu.make_async_copy(stage.at[me], heads_own.at[me], local_sem)
+    own.start()
+    for copy in loads + pairs:
+        copy.start()
+    early = up_in.shape[0] // 2 + down_in.shape[0] // 2
+    reducer = Reducer(
+        ((up_in, 0, up_in.shape[0] // 2), (down_in, 0, down_in.shape[0] // 2), (sums_ref, 0, sums_ref.shape[0] // 2)),
+        summed, buffers[:REDUCER_BUFFERS], buffers[REDUCER_BUFFERS:], lag, early, gap,
+    )
+    reducer.begin((0, 1))
+
+    def hand_on(step, carry):
+        block_copy(step).wait_recv()
+        relay(heads_own, step).start()
+        reducer.run((step - 1) * per_block, step * per_block)
+        return carry
+
+    lax.fori_loop(1, spans, hand_on, 0)
+    state = [(spans - 1) * per_block]
+
+    def advance(count):
+        stop = min(state[0] + count, early + gap)
+        reducer.run(state[0], stop)
+        state[0] = stop
+
+    own.wait()
+    for copy in loads:
+        copy.wait()
     low = lax.broadcasted_iota(jnp.int32, (tok, LANES), 1) < HEAD_DIM
-    for pair in range(HEADS // 2):
-        cols = slice(pair * LANES, (pair + 1) * LANES)
-        even, odd = heads_ref[2 * pair].astype(F32), heads_ref[2 * pair + 1].astype(F32)
-        att, gq = split_pair(even[:, :LANES], odd[:, :LANES], low)
-        gk, gv = split_pair(even[:, LANES:], odd[:, LANES:], low)
-        att_ref[:, cols] = att.astype(BF16)
-        gproj_ref[:, pair * LANES : (pair + 1) * LANES] = rotate_tile(gq, tables, -1.0).astype(BF16)
-        gproj_ref[:, width + pair * LANES : width + (pair + 1) * LANES] = rotate_tile(gk, tables, -1.0).astype(BF16)
-        gproj_ref[:, 2 * width + pair * LANES : 2 * width + (pair + 1) * LANES] = gv.astype(BF16)
+
+    def unpack(source, att_to, gproj_to):
+        for pair in range(HEADS // 2):
+            at = pair * LANES
+            even, odd = source[2 * pair].astype(F32), source[2 * pair + 1].astype(F32)
+            att, gq = split_pair(even[:, :LANES], odd[:, :LANES], low)
+            gk, gv = split_pair(even[:, LANES:], odd[:, LANES:], low)
+            att_to[:, at : at + LANES] = att.astype(BF16)
+            for part, grad in enumerate((gq, gk, gv)):
+                gproj_to[:, part * width + at : part * width + at + LANES] = grad.astype(BF16)
+
+    unpack(heads_own, att_ref, gproj_ref)
+    advance(1)
+    normed_tr[:, :tok] = normed_ref[...].T
+    normed_tr[:, tok:] = normed_peer[...].T
+    for copy in pairs:
+        copy.wait()
+    advance(1)
+    rows = x_ref[...].astype(F32)
+    branch = mlp_own[...].astype(F32) + mlp_other[...].astype(F32)
+    out_ref[...] = (rows + dot_nn(att_ref[...], wout_ref[...]) + branch + bias_ref[...]).astype(BF16)
+    advance(1)
+    grad_normed = dot_nt(gproj_ref[...], wqkv_ref[...]) + gn_own[...].astype(F32) + gn_other[...].astype(F32)
+    grad_in_ref[...] = grad_normed
+    advance(1)
     rows = x_ref[...].astype(F32)
     cot = cot_ref[...].astype(F32)
-    attn = dot_nn(att_ref[...], wout_ref[...])
-    branch = mlp_a[...].astype(F32) + mlp_b[...].astype(F32)
-    out_ref[...] = (rows + attn + branch + bias_ref[...]).astype(BF16)
-    grad_normed = dot_nt(gproj_ref[...], wqkv_ref[...]) + gn_a[...].astype(F32) + gn_b[...].astype(F32)
+    grad_normed = grad_in_ref[...]
     centre = jnp.mean(rows, axis=-1, keepdims=True)
     centred = rows - centre
     inv = lax.rsqrt(jnp.mean(centred * centred, axis=-1, keepdims=True) + EPSILON)
@@ -369,33 +729,136 @@
     small_ref[0:1, :] = jnp.sum(grad_normed * unit, axis=0, keepdims=True)
     small_ref[1:2, :] = jnp.sum(grad_normed, axis=0, keepdims=True)
     small_ref[2:3, :] = jnp.sum(cot, axis=0, keepdims=True)
-    bqkv_ref[...] = jnp.sum(gproj_ref[...].astype(F32), axis=0, keepdims=True)
+    for part in range(3):
+        part_cols = slice(part * width, (part + 1) * width)
+        small_ref[3 + part : 4 + part, :] = jnp.sum(gproj_ref[:, part_cols].astype(F32), axis=0, keepdims=True)
+    small_ref[6:7, :] = gbias_ref[:, :width]
+    small_ref[7:8, :] = gbias_ref[:, width:]
     grad_unit = grad_normed * gain_ref[...]
     grad_in_ref[...] = cot + inv * (
         grad_unit
         - jnp.mean(grad_unit, axis=-1, keepdims=True)
         - unit * jnp.mean(grad_unit * unit, axis=-1, keepdims=True)
     )
-
-
-def finish(heads, x, cot, gain, w_qkv, w_out, bias, mlp_parts, gn_parts, tables):
-    tok, width = x.shape
+    swap = to_peer(small_ref, landing, swap_send, swap_recv)
+    swap.start()
+    advance(1)
+    for step in range(spans):
+        relay(heads_own, step).wait()
+    unpack(heads_peer, att_peer, gproj_peer)
+    advance(1)
+    third, half, group = 3 * width // 2, width // 2, 512
+    for start in range(0, third, group):
+        cols = pl.ds(pl.multiple_of(here * third + start, LANES), group)
+        block, at = start // width, start % width
+        sums_ref[block * chunks : (block + 1) * chunks, :, at : at + group] = (
+            dot_nn(normed_tr[...], jnp.concatenate([gproj_ref[:, cols], gproj_peer[:, cols]], axis=0))
+            .astype(BF16).reshape(chunks, CHUNK, group)
+        )
+        advance(1)
+    cols = pl.ds(pl.multiple_of(here * half, LANES), half)
+    att_tr = jnp.concatenate([att_ref[...], att_peer[...]], axis=0).T
+    cots = jnp.concatenate([cot_ref[:, cols], cot_peer[:, cols]], axis=0)
+    sums_ref[chunks : 2 * chunks, :, half:] = dot_nn(att_tr, cots).astype(BF16).reshape(chunks, CHUNK, half)
+    swap.wait()
+    shared = lax.broadcasted_iota(jnp.int32, (8, width), 0) < 6
+    sums_ref[2 * chunks : 2 * chunks + 2] = jnp.zeros((2, CHUNK, width), BF16)
+    sums_ref[2 * chunks, 0:16, :] = jnp.concatenate(
+        [small_ref[...] + jnp.where(shared, landing[...], 0.0), jnp.zeros((8, width), F32)], axis=0
+    ).astype(BF16)
+    advance(early + gap)
+    reducer.begin((2,))
+    reducer.run(early + gap, reducer.ticks)
+    reducer.drain()
+    for step in range(1, spans):
+        block_copy(step).wait_send()
+
+
+def last(stage, mlp_give, gn_give, sum_up, sum_down, w_qkv, w_out, *operands):
+    spans = stage.shape[0]
+    tok, width = operands[0].shape
+    chunk = sum_up.shape[1:]
+    late = 2 * (width // CHUNK) + 2
+    total = (sum_up.shape[0] + sum_down.shape[0] + late) // 2
     vmem = pl.BlockSpec(memory_space=pltpu.VMEM)
+    any_spec = pl.BlockSpec(memory_space=pl.ANY)
+    tokens, wide = pltpu.VMEM((tok, width), BF16), pltpu.VMEM((tok, 3 * width), BF16)
     return pl.pallas_call(
-        finish_kernel,
+        functools.partial(last_kernel, TREE_LAG, TREE_GAP, TICKS_PER_BLOCK),
         out_shape=(
             jax.ShapeDtypeStruct((tok, width), BF16),
             jax.ShapeDtypeStruct((tok, width), F32),
-            jax.ShapeDtypeStruct((tok, width), BF16),
-            jax.ShapeDtypeStruct((tok, 3 * width), BF16),
-            jax.ShapeDtypeStruct((8, width), F32),
-            jax.ShapeDtypeStruct((1, 3 * width), F32),
+            jax.ShapeDtypeStruct((2 * total,) + chunk, BF16),
         ),
-        in_specs=[vmem] * 12,
-        out_specs=(vmem,) * 6,
-        compiler_params=pltpu.CompilerParams(vmem_limit_bytes=VMEM_BIG),
-        name="finish",
-    )(heads, x, cot, gain, w_qkv, w_out, bias, *mlp_parts, *gn_parts, tables)
+        in_specs=[any_spec] * 7 + [vmem] * len(operands),
+        out_specs=(vmem, vmem, any_spec),
+        scratch_shapes=[
+            pltpu.VMEM(stage.shape, BF16), pltpu.VMEM(stage.shape, BF16), tokens, tokens,
+            pltpu.VMEM(w_qkv.shape, BF16), pltpu.VMEM(w_out.shape, BF16), tokens, tokens, wide, wide,
+            pltpu.VMEM((width, 2 * tok), BF16), pltpu.VMEM((late,) + chunk, BF16),
+            pltpu.VMEM((8, width), F32), pltpu.VMEM((8, width), F32),
+        ]
+        + [pltpu.SemaphoreType.DMA((spans,))] * 4
+        + [pltpu.SemaphoreType.DMA((2,))] * 2
+        + [pltpu.SemaphoreType.DMA, pltpu.SemaphoreType.DMA((2,)), pltpu.SemaphoreType.DMA, pltpu.SemaphoreType.DMA]
+        + reducer_scratch(total, chunk),
+        compiler_params=pltpu.CompilerParams(
+            collective_id=1, has_side_effects=True, vmem_limit_bytes=VMEM_ALL
+        ),
+        name="last",
+    )(stage, mlp_give, gn_give, sum_up, sum_down, w_qkv, w_out, *operands)
+
+
+def widen_kernel(up_a, up_b, down_a, down_b, first_ref, second_ref, vec_ref, out_in, grad_in,
+                 qkv_ref, out_ref, up_ref, down_ref, vec_out, out_out, grad_out):
+    width = first_ref.shape[-1]
+    half = width // 2
+    qkv_ref[:, :width] = first_ref[0].astype(F32)
+    qkv_ref[:, width:] = second_ref[0, :, :half].astype(F32)
+    out_ref[...] = second_ref[0, :, half:].astype(F32)
+    up_ref[:, :width] = up_a[0].astype(F32)
+    up_ref[:, width:] = up_b[0].astype(F32)
+    down_ref[0] = down_a[0].astype(F32)
+    down_ref[1] = down_b[0].astype(F32)
+
+    @pl.when(pl.program_id(0) == 0)
+    def _():
+        vec_out[...] = vec_ref[0, :16, :].astype(F32)
+        out_out[...] = out_in[...]
+        grad_out[...] = grad_in[...]
+
+
+def widen(summed, output, grad_input):
+    chunk, width = summed.shape[1:]
+    steps = width // chunk
+    row = lambda cols: pl.BlockSpec((chunk, cols), lambda s: (s, 0))
+    blocks = [pl.BlockSpec((1, chunk, width), lambda s, n=n: (n * steps + s, 0, 0)) for n in range(6)]
+    const = lambda shape: pl.BlockSpec(shape, lambda s: (0,) * len(shape))
+    qkv, out, up, down, vec, output, grad_input = pl.pallas_call(
+        widen_kernel,
+        grid=(steps,),
+        out_shape=(
+            jax.ShapeDtypeStruct((width, 3 * width // 2), F32),
+            jax.ShapeDtypeStruct((width, width // 2), F32),
+            jax.ShapeDtypeStruct((width, 2 * width), F32),
+            jax.ShapeDtypeStruct((2, width, width), F32),
+            jax.ShapeDtypeStruct((16, width), F32),
+            jax.ShapeDtypeStruct(output.shape, BF16),
+            jax.ShapeDtypeStruct(grad_input.shape, F32),
+        ),
+        in_specs=blocks
+        + [
+            pl.BlockSpec((1, chunk, width), lambda s: (6 * steps, 0, 0)),
+            const(output.shape), const(grad_input.shape),
+        ],
+        out_specs=(
+            row(3 * width // 2), row(width // 2), row(2 * width),
+            pl.BlockSpec((2, chunk, width), lambda s: (0, s, 0)),
+            const((16, width)), const(output.shape), const(grad_input.shape),
+        ),
+        name="widen",
+    )(*[summed] * 7, output, grad_input)
+    return qkv, out, up, down.reshape(2 * width, width), vec, output, grad_input
 
 
 def by_heads(
@@ -415,59 +878,32 @@
 
     normed, send = project(x, cot, gain, shift, w_qkv, b_qkv[None], w_out, tables)
     heads, (normed_peer, cot_peer) = exchange(send, (normed, cot), 0)
-
-    normed_all = jnp.concatenate([normed, normed_peer])
-    cot_all = jnp.concatenate([cot, cot_peer])
-    up = dot_nn(normed_all, w_up) + b_up
-    erf_part = 0.5 * (1.0 + lax.erf(up * SQRT_HALF))
-    activated = (up * erf_part).astype(BF16)
-    slope = erf_part + up * jnp.exp(-0.5 * up * up) * INV_ROOT_TWO_PI
-    grad_up = (dot_nt(cot_all, w_down) * slope).astype(BF16)
-    mlp_part = dot_nn(activated, w_down).astype(BF16)
-    gn_part = dot_nt(grad_up, w_up).astype(BF16)
-    grad_w_down = dot_tn(activated, cot_all).astype(BF16)
-    grad_w_up = dot_tn(normed_all, grad_up).astype(BF16)
-    grad_b_up = jnp.sum(grad_up.astype(F32), axis=0).astype(BF16)
-
-    done = attention(heads, order)
-    back, (mlp_other, gn_other) = exchange(done, (mlp_part[tok:], gn_part[tok:]), 1)
-    output, grad_input, attended, grad_project, small, grad_b_qkv = finish(
-        back, x, cot, gain, w_qkv, w_out, (b_out + b_down)[None],
-        (mlp_part[:tok], mlp_other), (gn_part[:tok], gn_other), tables,
-    )
-    third = 3 * width // 2
-    gp_here = lax.dynamic_slice_in_dim(grad_project, seq_here * third, third, axis=1)
-    gp_give = lax.dynamic_slice_in_dim(grad_project, (1 - seq_here) * third, third, axis=1)
-    att_peer, gp_peer = swap((attended, gp_give), 2)
-    cot_cols = lax.dynamic_slice_in_dim(cot_all, seq_here * (width // 2), width // 2, axis=1)
-    grad_w_qkv = dot_tn(normed_all, jnp.concatenate([gp_here, gp_peer])).astype(BF16)
-    grad_w_out = dot_tn(jnp.concatenate([attended, att_peer]), cot_cols).astype(BF16)
-
-    everyone = ("dp", "mlp")
-    vec = jnp.concatenate([small[0], small[1], small[2], grad_b_qkv[0]])
-    vec, b_up_sum, s_qkv, s_out, s_up, s_down = (
-        lax.psum(vec, everyone),
-        lax.psum(grad_b_up, "dp"),
-        lax.psum(grad_w_qkv, "dp"),
-        lax.psum(grad_w_out, "dp"),
-        lax.psum(grad_w_up, "dp"),
-        lax.psum(grad_w_down, "dp"),
-    )
+    mlp_part, mlp_give, gn_part, gn_give, sum_up, sum_down, grad_b_up = feed_forward(
+        normed, normed_peer, cot, cot_peer, w_up, b_up[None], w_down
+    )
+    stage = attention(heads, order, offsets)
+    output, grad_input, summed = last(
+        stage, mlp_give, gn_give, sum_up, sum_down, w_qkv, w_out,
+        x, cot, cot_peer, normed, normed_peer, gain, (b_out + b_down)[None], mlp_part, gn_part, grad_b_up,
+    )
+    qkv, out, up, down, vec, output, grad_input = widen(summed, output, grad_input)
     half = width // 2
-    piece = lambda start, size: lax.dynamic_slice_in_dim(vec, start + seq_here * size, size)
-    bias_sum = piece(2 * width, half)
+    piece = lambda start, rows: lax.dynamic_slice_in_dim(
+        vec[start : start + rows].reshape(-1), seq_here * (rows * half), rows * half
+    )
+    bias_sum = piece(2, 1)
     return (
         output.reshape(1, 1, tok, width),
         grad_input.reshape(1, 1, tok, width),
-        piece(0, half),
-        piece(width, half),
-        s_qkv.astype(F32),
-        piece(3 * width, third),
-        s_out.astype(F32),
+        piece(0, 1),
+        piece(1, 1),
+        qkv,
+        piece(3, 3),
+        out,
         bias_sum,
-        s_up.astype(F32),
-        b_up_sum.astype(F32),
-        s_down.astype(F32),
+        up,
+        vec[6:8].reshape(-1),
+        down,
         bias_sum,
     )
 

time: 453 us -> 312 us (0.69)
  waiting for transfers between devices: 158 us -> 0 us
  Pallas kernels: 143 us -> 300 us
  blocking collectives: 81.1 us -> 0 us
  matrix products: 25.6 us -> 0 us
  other arithmetic: 19.4 us -> 3.39 us
  between operations: 15 us -> 1.43 us
    pallas_call x2 -> x3, Pallas kernels: 28.9 us -> 219 us  [the longest x1 184 us: last(): pl.pallas_call(functools.partial(last_kernel, TREE_LAG, TREE_GAP, TICKS_P...]
    psum x1 -> x0, waiting for transfers between devices: 158 us -> none  [by_heads(): lax.psum(grad_w_qkv, 'dp')]
    psum x2 -> x0, blocking collectives: 81.1 us -> none  [the longest x1 48.7 us: by_heads(): lax.psum(vec, everyone)]
    pallas_call x2 -> x1, Pallas kernels: 61.4 us -> 28.3 us  [exchange(): pl.pallas_call(functools.partial(exchange_kernel, count, peers, None), ou...]
    dot_general x8 -> x0, matrix products: 25.6 us -> none  [the longest x4 15.1 us: dot_tn(): lax.dot_general(a, b, (((0,), (0,)), ((), ())), preferred_element_type=F32)]
    convert_element_type x5 -> x0, other arithmetic: 17 us -> none  [the longest x1 6.8 us: by_heads(): s_up.astype(F32)]
  transfers between devices with their start and end apart: 1 -> 0, of which waited for: 1 -> 0; matrix products, arithmetic and copies ran while one was open for 1% -> 0% of each run, Pallas kernels for 0% -> 0%
where the time goes in v3:
time: 312 us; the launch traced here: 311 us
  Pallas kernels  300 us (96%)
  local copies, waits for them, and re-layouts  6.75 us (2%)
  other arithmetic  3.39 us (1%)
    pallas_call x1, Pallas kernels, last(): pl.pallas_call(functools.partial(last_kernel, TREE_LAG, TREE_GAP, TICKS_P...  184 us
    pallas_call x1, Pallas kernels, attention(): pl.pallas_call(functools.partial(attention_kernel, tile), out_shape=jax.S...  45.7 us
    pallas_call x1, Pallas kernels, exchange(): pl.pallas_call(functools.partial(exchange_kernel, count, peers, None), ou...  28.3 us
    pallas_call x1, Pallas kernels, widen(): pl.pallas_call(widen_kernel, grid=(steps,), out_shape=(jax.ShapeDtypeStru...  17.6 us
    pallas_call x1, Pallas kernels, feed_forward(): pl.pallas_call(feed_forward_kernel, grid=(steps,), out_shape=(jax.ShapeDt...  16.8 us
    pallas_call x1, Pallas kernels, project(): pl.pallas_call(project_kernel, grid=(steps,), out_shape=(jax.ShapeDtypeSt...  7.1 us

profile of v3, /device:TPU:0, one launch (start us, length us, event | category | flops | bytes accessed | tf_op | source)
XLA Modules:
  0.0 311.3 jit_solution(3773869812139590863)
XLA Ops:
  0.7 1.3 dynamic_slice.27
  2.6 0.4 fusion.3
  3.0 0.7 pad_maximum_fusion.tab_ref
  3.7 7.1 %project.1 = (bf16[160,1024]{1,0:T(8,128)(2,1)}, bf16[16,160,256]{2,1,0:T(8,128)(2,1)}) custom-call(bf16[160,1024]{1,0:T(8,128)(2,1)} %bitcast.25, bf16[160,1024]{1,0:T(8,128)(2,1)} %bitcast.21, f32[1,1024]{1,0:T(1,128)} %bitcast.30, f32[1,1024]{1,0:T(1,128)} %bitcast.37, bf16[1024,3072]{1,0:T(8,128)(2,1)} %wqkv_hbm.1, bf16[1024,3072]{1,0:T(8,128)(2,1)} %wqkv_hbm.1, ...), custom_call_target="tpu_custom_call" | custom-call | tf_op jit(solution)/shard_map/project/pallas_call | solution.py:109
  10.8 28.3 %exchange0.1 = (bf16[16,160,256]{2,1,0:T(8,128)(2,1)}, bf16[160,1024]{1,0:T(8,128)(2,1)}, bf16[160,1024]{1,0:T(8,128)(2,1)}) custom-call(bf16[16,160,256]{2,1,0:T(8,128)(2,1)} %get-tuple-element.34.refs_0_, bf16[160,1024]{1,0:T(8,128)(2,1)} %get-tuple-element.35.refs_1_.normed_a.normed_ref, bf16[160,1024]{1,0:T(8,128)(2,1)} %bitcast.22), custom_call_target="tpu_custom_call" | custom-call | tf_op jit(solution)/shard_map/exchange0/pallas_call | solution.py:174
  39.1 0.0 copy-start.3
  39.1 16.8 %feed_forward.1 = (bf16[160,1024]{1,0:T(8,128)(2,1)}, bf16[160,1024]{1,0:T(8,128)(2,1)}, bf16[160,1024]{1,0:T(8,128)(2,1)}, bf16[160,1024]{1,0:T(8,128)(2,1)}, b...) custom-call(bf16[160,1024]{1,0:T(8,128)(2,1)} %get-tuple-element.35.refs_1_.normed_a.normed_ref, ...), custom_call_target="tpu_custom_call" | custom-call | tf_op jit(solution)/shard_map/feed_forward/pallas_call | solution.py:241
  55.9 0.0 copy-done.3
  55.9 0.0 copy-start.4
  56.0 0.6 select_reduce_fusion.order_ref
  56.6 0.4 fusion.5
  57.0 0.7 pad_maximum_fusion.1.angle_ref
  57.6 0.0 copy-done.4
  57.6 0.0 copy-start.1
  57.6 0.0 copy-start.2
  57.6 45.7 %attention.1.stage = bf16[16,160,256]{2,1,0:T(8,128)(2,1)} custom-call(s32[16]{0:T(128)} %select_reduce_fusion.order_ref, s32[16]{0:T(128)} %copy-done.4, bf16[16,160,256]{2,1,0:T(8,128)(2,1)} %get-tuple-element.36.in_ref, f32[2,8,2560]{2,1,0:T(8,128)} %pad_maximum_fusion.1.angle_ref), custom_call_target="tpu_custom_call" | custom-call | flops 40000000000 | bytes 10000000 | tf_op jit(solution)/shard_map/attention/pallas_call | solution.py:607
  103.3 0.0 copy-done.1
  103.3 0.0 copy-done.2
  103.3 0.6 add.61
  103.9 184.3 %last.1 = (bf16[160,1024]{1,0:T(8,128)(2,1)}, f32[160,1024]{1,0:T(8,128)}, bf16[98,64,1024]{2,1,0:T(8,128)(2,1)}) custom-call(bf16[16,160,256]{2,1,0:T(8,128)(2,1)} %attention.1.stage, bf16[160,1024]{1,0:T(8,128)(2,1)} %get-tuple-element.39.mlp_in, bf16[160,1024]{1,0:T(8,128)(2,1)} %get-tuple-element.40.gn_in, ...), custom_call_target="tpu_custom_call" | custom-call | tf_op jit(solution)/shard_map/last/pallas_call | solution.py:786
  288.2 17.6 %widen.1 = (f32[1024,1536]{1,0:T(8,128)}, f32[1024,512]{1,0:T(8,128)}, f32[1024,2048]{1,0:T(8,128)}, f32[2,1024,1024]{2,1,0:T(8,128)}, f32[16,1024]{1,0:T(8,128)...) custom-call(bf16[98,64,1024]{2,1,0:T(8,128)(2,1)} %get-tuple-element.46.up_a.up_b.down_a.down_b.first_ref.second_ref.vec_ref, ...), custom_call_target="tpu_custom_call" | custom-call | tf_op jit(solution)/shard_map/widen/pallas_call | solution.py:837
  305.8 0.8 slice.17
  306.6 0.7 dynamic_slice.32
  307.3 0.9 fusion.12
  308.2 0.0 copy-start
  308.2 0.6 constant_dynamic-slice_fusion
  308.8 0.6 constant_dynamic-slice_fusion.1
  309.4 0.8 slice_bitcast_fusion
  310.1 0.6 copy.27
  310.7 0.6 copy.29
  311.3 0.0 copy-done
  (8 shorter events, 0.1 us)
Async XLA Ops:
  39.1 16.8 %copy-start.3 = (s32[16,2]{0,1:T(2,128)S(1)}, s32[16,2]{0,1:T(2,128)}, u32[]{:S(2)}) copy-start(s32[16,2]{0,1:T(2,128)} %param.14) | copy-start | bytes 388
  55.9 1.7 copy-start.4
  57.6 45.7 %copy-start.1 = (f32[1024]{0:T(1024)S(1)}, f32[1024]{0:T(1024)}, u32[]{:S(2)}) copy-start(f32[1024]{0:T(1024)} %param.20) | copy-start | bytes 12292
  57.6 45.7 %copy-start.2 = (f32[1024]{0:T(1024)S(1)}, f32[1024]{0:T(1024)}, u32[]{:S(2)}) copy-start(f32[1024]{0:T(1024)} %param.24) | copy-start | bytes 12292
  308.2 3.1 %copy-start = (f32[1,512]{1,0:T(1,128)}, f32[1,512]{1,0:T(1,128)S(1)}, u32[]{:S(2)}) copy-start(f32[1,512]{1,0:T(1,128)S(1)} %constant_dynamic-slice_fusion.2) | copy-start | bytes 6148

commit v4 on v3

--- a/solution.py
+++ b/solution.py
@@ -23,7 +23,7 @@
 LANES = 128
 VMEM_BIG = 60 * 1024 * 1024
 TREE_LAG = 4
-TREE_GAP = 12
+TREE_GAP = 4
 TICKS_PER_BLOCK = 2
 VMEM_ALL = 66 * 1024 * 1024 - 2**20 // 2
 
@@ -127,148 +127,135 @@
     )(x, cot, gain, shift, w_qkv, w_qkv, w_qkv, b_qkv, b_qkv, b_qkv, w_out, tables)
 
 
-def exchange_kernel(count, peers, blocks, *refs):
-    heads_in, rest = refs[0], refs[1:]
-    pairs_in, rest = rest[:count], rest[count:]
-    heads_out, rest = rest[0], rest[1:]
-    pairs_out, rest = rest[:count], rest[count:]
-    head_send, head_recv, pair_send, pair_recv, local_sem = rest
+def greet(barrier, peers):
     me = lax.axis_index("dp")
-    other = 1 - lax.axis_index("mlp")
-    barrier = pltpu.get_barrier_semaphore()
     for step in range(1, peers):
         pl.semaphore_signal(barrier, inc=1, device_id={"dp": lax.rem(me + step, peers)}, device_id_type=MESH)
-    if count:
-        pl.semaphore_signal(barrier, inc=1, device_id={"mlp": other}, device_id_type=MESH)
-    pl.semaphore_wait(barrier, peers - 1 + (1 if count else 0))
-    copies = []
-    for i in range(count):
-        copies.append(
-            pltpu.make_async_remote_copy(
-                src_ref=pairs_in[i], dst_ref=pairs_out[i], send_sem=pair_send.at[i], recv_sem=pair_recv.at[i],
-                device_id={"mlp": other}, device_id_type=MESH,
-            )
-        )
-    for step in range(1, peers):
-        target = lax.rem(me + step, peers)
-        copies.append(
-            pltpu.make_async_remote_copy(
-                src_ref=heads_in.at[target], dst_ref=heads_out.at[me],
-                send_sem=head_send.at[step], recv_sem=head_recv.at[step],
-                device_id={"dp": target}, device_id_type=MESH,
-            )
-        )
-    for copy in copies:
+    pl.semaphore_signal(barrier, inc=1, device_id={"mlp": 1 - lax.axis_index("mlp")}, device_id_type=MESH)
+    pl.semaphore_wait(barrier, peers)
+
+
+def to_peer(src, dst, send, recv):
+    return pltpu.make_async_remote_copy(
+        src_ref=src, dst_ref=dst, send_sem=send, recv_sem=recv,
+        device_id={"mlp": 1 - lax.axis_index("mlp")}, device_id_type=MESH,
+    )
+
+
+CHUNK = 64
+
+
+def first_kernel(
+    group, heads_in, normed_ref, cot_ref, wup_hbm, wdown_hbm, bup_ref,
+    heads_out, normed_peer, cot_peer, mlp_ref, mlp_give, gn_ref, gn_give, up_out, down_out, gbias_ref,
+    wup_ref, wdown_ref, normed_all, normed_tr, cot_all, mlp_acc, gn_acc, up_sum, down_sum,
+    head_send, head_recv, pair_send, pair_recv, local_sem, load_sem, store_sem,
+):
+    spans = heads_in.shape[0]
+    tok, width = normed_ref.shape
+    hidden = wup_ref.shape[1]
+    me = lax.axis_index("dp")
+    greet(pltpu.get_barrier_semaphore(), spans)
+    pairs = [
+        to_peer(src, dst, pair_send.at[n], pair_recv.at[n])
+        for n, (src, dst) in enumerate(((normed_ref, normed_peer), (cot_ref, cot_peer)))
+    ]
+    loads = [
+        pltpu.make_async_copy(src, dst, load_sem.at[n])
+        for n, (src, dst) in enumerate(((wup_hbm, wup_ref), (wdown_hbm, wdown_ref)))
+    ]
+
+    def block_copy(step):
+        target = lax.rem(me + step, spans)
+        return pltpu.make_async_remote_copy(
+            src_ref=heads_in.at[target], dst_ref=heads_out.at[me], send_sem=head_send.at[step],
+            recv_sem=head_recv.at[step], device_id={"dp": target}, device_id_type=MESH,
+        )
+
+    for copy in pairs + loads:
         copy.start()
+    for step in range(1, spans):
+        block_copy(step).start()
     own = pltpu.make_async_copy(heads_in.at[me], heads_out.at[me], local_sem)
     own.start()
+    normed_all[:tok, :] = normed_ref[...]
+    normed_tr[:, :tok] = normed_ref[...].T
+    cot_all[:tok, :] = cot_ref[...]
+    mlp_acc[...] = jnp.zeros_like(mlp_acc)
+    gn_acc[...] = jnp.zeros_like(gn_acc)
+    for copy in loads + pairs:
+        copy.wait()
+    normed_all[tok:, :] = normed_peer[...]
+    normed_tr[:, tok:] = normed_peer[...].T
+    cot_all[tok:, :] = cot_peer[...]
+    per = width // group
+
+    def body(step, carry):
+        hid = pl.ds(pl.multiple_of(step * group, group), group)
+        at = pl.ds(pl.multiple_of(lax.rem(step, per) * group, group), group)
+        w_up, w_down = wup_ref[:, hid], wdown_ref[hid, :]
+        up = dot_nn(normed_all[...], w_up) + bup_ref[:, hid]
+        half_erf = 0.5 * (1.0 + lax.erf(up * SQRT_HALF))
+        activated = (up * half_erf).astype(BF16)
+        slope = half_erf + up * jnp.exp(-0.5 * up * up) * INV_ROOT_TWO_PI
+        grad_up = (dot_nt(cot_all[...], w_down) * slope).astype(BF16)
+        mlp_acc[...] += dot_nn(activated, w_down)
+        gn_acc[...] += dot_nt(grad_up, w_up)
+        up_sum[pl.ds(step // per * (width // CHUNK), width // CHUNK), :, at] = (
+            dot_nn(normed_tr[...], grad_up).astype(BF16).reshape(width // CHUNK, CHUNK, group)
+        )
+        down_sum[pl.ds(step * (group // CHUNK), group // CHUNK)] = (
+            dot_nn(activated.T, cot_all[...]).astype(BF16).reshape(group // CHUNK, CHUNK, width)
+        )
+        gbias_ref[:, hid] = jnp.sum(grad_up.astype(F32), axis=0, keepdims=True)
+        return carry
+
+    lax.fori_loop(0, hidden // group, body, 0)
+    stores = [
+        pltpu.make_async_copy(src, dst, store_sem.at[n])
+        for n, (src, dst) in enumerate(((up_sum, up_out), (down_sum, down_out)))
+    ]
+    for copy in stores:
+        copy.start()
+    mlp_ref[...] = mlp_acc[:tok, :].astype(BF16)
+    mlp_give[...] = mlp_acc[tok:, :].astype(BF16)
+    gn_ref[...] = gn_acc[:tok, :].astype(BF16)
+    gn_give[...] = gn_acc[tok:, :].astype(BF16)
     own.wait()
-    for copy in copies:
+    for step in range(1, spans):
+        block_copy(step).wait()
+    for copy in stores:
         copy.wait()
 
 
-def exchange(heads, pairs, collective):
-    count = len(pairs)
-    peers = heads.shape[0]
-    any_spec = pl.BlockSpec(memory_space=pl.ANY)
-    out = pl.pallas_call(
-        functools.partial(exchange_kernel, count, peers, None),
-        out_shape=(jax.ShapeDtypeStruct(heads.shape, heads.dtype),)
-        + tuple(jax.ShapeDtypeStruct(p.shape, p.dtype) for p in pairs),
-        in_specs=[any_spec] * (1 + count),
-        out_specs=(any_spec,) * (1 + count),
-        scratch_shapes=[
-            pltpu.SemaphoreType.DMA((peers,)),
-            pltpu.SemaphoreType.DMA((peers,)),
-            pltpu.SemaphoreType.DMA((max(count, 1),)),
-            pltpu.SemaphoreType.DMA((max(count, 1),)),
-            pltpu.SemaphoreType.DMA,
-        ],
-        compiler_params=pltpu.CompilerParams(collective_id=collective, has_side_effects=True),
-        name="exchange" + str(collective),
-    )(heads, *pairs)
-    return out[0], out[1:]
-
-
-CHUNK = 64
-
-
-def feed_forward_kernel(
-    normed_a, normed_b, cot_a, cot_b, wup_ref, bup_ref, wdown_ref,
-    mlp_ref, mlp_give, gn_ref, gn_give, gup_ref, gdown_ref, gbias_ref,
-    normed_all, normed_tr, cot_all, mlp_acc, gn_acc,
-):
-    step = pl.program_id(0)
-    tok = normed_a.shape[0]
-
-    @pl.when(step == 0)
-    def _():
-        for ref, parts in ((normed_all, (normed_a, normed_b)), (cot_all, (cot_a, cot_b))):
-            ref[:tok, :] = parts[0][...]
-            ref[tok:, :] = parts[1][...]
-        normed_tr[...] = normed_all[...].T
-        mlp_acc[...] = jnp.zeros_like(mlp_acc)
-        gn_acc[...] = jnp.zeros_like(gn_acc)
-
-    w_up, w_down = wup_ref[...], wdown_ref[...]
-    up = dot_nn(normed_all[...], w_up) + bup_ref[...]
-    half_erf = 0.5 * (1.0 + lax.erf(up * SQRT_HALF))
-    activated = (up * half_erf).astype(BF16)
-    slope = half_erf + up * jnp.exp(-0.5 * up * up) * INV_ROOT_TWO_PI
-    grad_up = (dot_nt(cot_all[...], w_down) * slope).astype(BF16)
-    mlp_acc[...] += dot_nn(activated, w_down)
-    gn_acc[...] += dot_nt(grad_up, w_up)
-    gup_ref[...] = dot_nn(normed_tr[...], grad_up).astype(BF16).reshape(gup_ref.shape)
-    gdown_ref[...] = dot_nn(activated.T, cot_all[...]).astype(BF16).reshape(gdown_ref.shape)
-    gbias_ref[...] = jnp.sum(grad_up.astype(F32), axis=0, keepdims=True)
-
-    @pl.when(step == pl.num_programs(0) - 1)
-    def _():
-        mlp_ref[...] = mlp_acc[:tok, :].astype(BF16)
-        mlp_give[...] = mlp_acc[tok:, :].astype(BF16)
-        gn_ref[...] = gn_acc[:tok, :].astype(BF16)
-        gn_give[...] = gn_acc[tok:, :].astype(BF16)
-
-
-def feed_forward(normed, normed_peer, cot, cot_peer, w_up, b_up, w_down):
+def first(heads, normed, cot, w_up, w_down, b_up):
+    spans = heads.shape[0]
     tok, width = normed.shape
     hidden = w_up.shape[1]
-    group = 256
-    steps = hidden // group
-    per = width // group
-    const = lambda shape: pl.BlockSpec(shape, lambda s: (0,) * len(shape))
-    chunks = hidden // CHUNK
+    vmem = pl.BlockSpec(memory_space=pltpu.VMEM)
+    any_spec = pl.BlockSpec(memory_space=pl.ANY)
+    tokens = jax.ShapeDtypeStruct((tok, width), BF16)
+    sums = (hidden // CHUNK, CHUNK, width)
+    both = (2 * tok, width)
     return pl.pallas_call(
-        feed_forward_kernel,
-        grid=(steps,),
-        out_shape=(jax.ShapeDtypeStruct((tok, width), BF16),) * 4
-        + (
-            jax.ShapeDtypeStruct((chunks, CHUNK, width), BF16),
-            jax.ShapeDtypeStruct((chunks, CHUNK, width), BF16),
-            jax.ShapeDtypeStruct((1, hidden), F32),
-        ),
-        in_specs=[const((tok, width))] * 4
-        + [
-            pl.BlockSpec((width, group), lambda s: (0, s)),
-            pl.BlockSpec((1, group), lambda s: (0, s)),
-            pl.BlockSpec((group, width), lambda s: (s, 0)),
-        ],
-        out_specs=(const((tok, width)),) * 4
-        + (
-            pl.BlockSpec((width // CHUNK, CHUNK, group), lambda s: (s // per, 0, s % per)),
-            pl.BlockSpec((group // CHUNK, CHUNK, width), lambda s: (s, 0, 0)),
-            pl.BlockSpec((1, group), lambda s: (0, s)),
-        ),
+        functools.partial(first_kernel, 256),
+        out_shape=(jax.ShapeDtypeStruct(heads.shape, BF16),) + (tokens,) * 6
+        + (jax.ShapeDtypeStruct(sums, BF16),) * 2
+        + (jax.ShapeDtypeStruct((1, hidden), F32),),
+        in_specs=[any_spec, vmem, vmem, any_spec, any_spec, vmem],
+        out_specs=(any_spec,) + (vmem,) * 6 + (any_spec,) * 2 + (vmem,),
         scratch_shapes=[
-            pltpu.VMEM((2 * tok, width), BF16),
-            pltpu.VMEM((width, 2 * tok), BF16),
-            pltpu.VMEM((2 * tok, width), BF16),
-            pltpu.VMEM((2 * tok, width), F32),
-            pltpu.VMEM((2 * tok, width), F32),
-        ],
-        compiler_params=pltpu.CompilerParams(vmem_limit_bytes=VMEM_BIG),
-        name="feed_forward",
-    )(normed, normed_peer, cot, cot_peer, w_up, b_up, w_down)
+            pltpu.VMEM(w_up.shape, BF16), pltpu.VMEM(w_down.shape, BF16),
+            pltpu.VMEM(both, BF16), pltpu.VMEM((width, 2 * tok), BF16), pltpu.VMEM(both, BF16),
+            pltpu.VMEM(both, F32), pltpu.VMEM(both, F32), pltpu.VMEM(sums, BF16), pltpu.VMEM(sums, BF16),
+        ]
+        + [pltpu.SemaphoreType.DMA((spans,))] * 2
+        + [pltpu.SemaphoreType.DMA((2,))] * 2
+        + [pltpu.SemaphoreType.DMA]
+        + [pltpu.SemaphoreType.DMA((2,))] * 2,
+        compiler_params=pltpu.CompilerParams(collective_id=0, has_side_effects=True, vmem_limit_bytes=VMEM_BIG),
+        name="first",
+    )(heads, normed, cot, w_up, w_down, b_up)
 
 
 TREE_PERIOD = 10
@@ -481,21 +468,6 @@
 REDUCER_BUFFERS, REDUCER_REFS = 6, 20
 
 
-def greet(barrier, peers):
-    me = lax.axis_index("dp")
-    for step in range(1, peers):
-        pl.semaphore_signal(barrier, inc=1, device_id={"dp": lax.rem(me + step, peers)}, device_id_type=MESH)
-    pl.semaphore_signal(barrier, inc=1, device_id={"mlp": 1 - lax.axis_index("mlp")}, device_id_type=MESH)
-    pl.semaphore_wait(barrier, peers)
-
-
-def to_peer(src, dst, send, recv):
-    return pltpu.make_async_remote_copy(
-        src_ref=src, dst_ref=dst, send_sem=send, recv_sem=recv,
-        device_id={"mlp": 1 - lax.axis_index("mlp")}, device_id_type=MESH,
-    )
-
-
 def attention_kernel(
     tile, order_ref, place_ref, in_ref, angle_ref, stage,
     q_nat, k_nat, v_nat, k_tr, v_tr, g_tr, probs, kv_grad, aq_out,
@@ -528,9 +500,8 @@
 
     lax.fori_loop(0, blocks, flip, 0)
 
-    key_row = lax.broadcasted_iota(jnp.int32, (tile, tile), 0)
-    query_col = lax.broadcasted_iota(jnp.int32, (tile, tile), 1)
-    causal = key_row <= query_col
+    tall = 2 * tile
+    ahead = lax.broadcasted_iota(jnp.int32, (tall, tile), 0) - lax.broadcasted_iota(jnp.int32, (tall, tile), 1)
     pad = jnp.zeros((tile, HEAD_DIM), BF16)
     half_rot = ROT // 2
 
@@ -544,20 +515,22 @@
         queries_pad = q_nat[q_rows, :]
         queries = queries_pad[:, :HEAD_DIM]
 
+        final = block // 2
+
         def forward(j, state, masked):
             mixed, totals = state
-            rows = pl.ds(pl.multiple_of(j * tile, tile), tile)
+            rows = pl.ds(pl.multiple_of(j * tall, tall), tall)
             prob = jnp.exp(dot_nt(k_nat[rows, :], queries))
             if masked:
-                prob = jnp.where(causal, prob, 0.0)
+                prob = jnp.where(ahead <= block * tile - j * tall, prob, 0.0)
             probs[rows, :] = prob
             mixed = mixed + dot_nn(v_tr[:, rows], prob.astype(BF16))
-            totals = totals + jnp.sum(prob.reshape(tile // 8, 8, tile), axis=0)
+            totals = totals + jnp.sum(prob.reshape(tall // 8, 8, tile), axis=0)
             return mixed, totals
 
         state = (jnp.zeros((HEAD_DIM, tile), F32), jnp.zeros((8, tile), F32))
-        state = lax.fori_loop(0, block, lambda j, s: forward(j, s, False), state)
-        mixed, totals = forward(block, state, True)
+        state = lax.fori_loop(0, final, lambda j, s: forward(j, s, False), state)
+        mixed, totals = forward(final, state, True)
         totals = jnp.sum(totals, axis=0, keepdims=True)
         attended = mixed / totals
         grad_att = g_tr[:, q_rows].astype(F32)
@@ -566,13 +539,13 @@
         grad_pad = jnp.concatenate([pad, grad_mixed.T], axis=1)
 
         def backward(j, grad_q):
-            rows = pl.ds(pl.multiple_of(j * tile, tile), tile)
+            rows = pl.ds(pl.multiple_of(j * tall, tall), tall)
             prob = probs[rows, :]
             grad_scores = (prob * (dot_nn(v_nat[rows, :], grad_mixed) + grad_totals)).astype(BF16)
             kv_grad[rows, :] += dot_nn(grad_scores, queries_pad) + dot_nn(prob.astype(BF16), grad_pad)
             return grad_q + dot_nn(k_tr[:, rows], grad_scores)
 
-        grad_q = lax.fori_loop(0, block + 1, backward, jnp.zeros((HEAD_DIM, tile), F32))
+        grad_q = lax.fori_loop(0, final + 1, backward, jnp.zeros((HEAD_DIM, tile), F32))
         aq_out[q_rows, :] = jnp.concatenate([attended, turn_back(grad_q * scale, q_rows)], axis=0).T.astype(BF16)
         return carry
 
@@ -877,9 +850,8 @@
     gain, shift = ln_gain[None], ln_bias[None]
 
     normed, send = project(x, cot, gain, shift, w_qkv, b_qkv[None], w_out, tables)
-    heads, (normed_peer, cot_peer) = exchange(send, (normed, cot), 0)
-    mlp_part, mlp_give, gn_part, gn_give, sum_up, sum_down, grad_b_up = feed_forward(
-        normed, normed_peer, cot, cot_peer, w_up, b_up[None], w_down
+    heads, normed_peer, cot_peer, mlp_part, mlp_give, gn_part, gn_give, sum_up, sum_down, grad_b_up = first(
+        send, normed, cot, w_up, w_down, b_up[None]
     )
     stage = attention(heads, order, offsets)
     output, grad_input, summed = last(

time: 312 us -> 280 us (0.90)
  Pallas kernels: 300 us -> 267 us
    pallas_call x1, Pallas kernels: 184 us -> 168 us  [last(): pl.pallas_call(functools.partial(last_kernel, TREE_LAG, TREE_GAP, TICKS_P...]
    pallas_call x1, Pallas kernels: 45.7 us -> 32.9 us  [attention(): pl.pallas_call(functools.partial(attention_kernel, tile), out_shape=jax.S...]
    pallas_call x2 -> x1, Pallas kernels: 45.1 us -> 41.3 us  [first(): pl.pallas_call(functools.partial(first_kernel, 256), out_shape=(jax.Shape...]
where the time goes in v4:
time: 280 us; the launch traced here: 279 us
  Pallas kernels  267 us (95%)
  local copies, waits for them, and re-layouts  6.85 us (2%)
  other arithmetic  3.41 us (1%)
    pallas_call x1, Pallas kernels, last(): pl.pallas_call(functools.partial(last_kernel, TREE_LAG, TREE_GAP, TICKS_P...  168 us
    pallas_call x1, Pallas kernels, first(): pl.pallas_call(functools.partial(first_kernel, 256), out_shape=(jax.Shape...  41.3 us
    pallas_call x1, Pallas kernels, attention(): pl.pallas_call(functools.partial(attention_kernel, tile), out_shape=jax.S...  32.9 us
    pallas_call x1, Pallas kernels, widen(): pl.pallas_call(widen_kernel, grid=(steps,), out_shape=(jax.ShapeDtypeStru...  17.6 us
    pallas_call x1, Pallas kernels, project(): pl.pallas_call(project_kernel, grid=(steps,), out_shape=(jax.ShapeDtypeSt...  7.1 us

profile of v4, /device:TPU:0, one launch (start us, length us, event | category | flops | bytes accessed | tf_op | source)
XLA Modules:
  0.0 278.6 jit_solution(5781238038266317252)
XLA Ops:
  0.7 1.3 dynamic_slice.27
  2.6 0.4 fusion.3
  3.0 0.7 pad_maximum_fusion.tab_ref
  3.7 7.1 %project.1 = (bf16[160,1024]{1,0:T(8,128)(2,1)}, bf16[16,160,256]{2,1,0:T(8,128)(2,1)}) custom-call(bf16[160,1024]{1,0:T(8,128)(2,1)} %bitcast.24, bf16[160,1024]{1,0:T(8,128)(2,1)} %bitcast.21, f32[1,1024]{1,0:T(1,128)} %bitcast.29, f32[1,1024]{1,0:T(1,128)} %bitcast.36, bf16[1024,3072]{1,0:T(8,128)(2,1)} %wqkv_hbm.1, bf16[1024,3072]{1,0:T(8,128)(2,1)} %wqkv_hbm.1, ...), custom_call_target="tpu_custom_call" | custom-call | tf_op jit(solution)/shard_map/project/pallas_call | solution.py:109
  10.8 0.0 copy-start.3
  10.8 41.3 %first.1 = (bf16[16,160,256]{2,1,0:T(8,128)(2,1)}, bf16[160,1024]{1,0:T(8,128)(2,1)}, bf16[160,1024]{1,0:T(8,128)(2,1)}, bf16[160,1024]{1,0:T(8,128)(2,1)}, bf16...) custom-call(bf16[16,160,256]{2,1,0:T(8,128)(2,1)} %get-tuple-element, ...), custom_call_target="tpu_custom_call" | custom-call | tf_op jit(solution)/shard_map/first/pallas_call | solution.py:240
  52.2 0.0 copy-done.3
  52.2 0.0 copy-start.4
  52.2 0.6 select_reduce_fusion.order_ref
  52.8 0.4 fusion.5
  53.2 0.7 pad_maximum_fusion.1.angle_ref
  53.9 0.0 copy-done.4
  53.9 0.0 copy-start.1
  53.9 0.0 copy-start.2
  53.9 32.9 %attention.1.stage = bf16[16,160,256]{2,1,0:T(8,128)(2,1)} custom-call(s32[16]{0:T(128)} %select_reduce_fusion.order_ref, s32[16]{0:T(128)} %copy-done.4, bf16[16,160,256]{2,1,0:T(8,128)(2,1)} %get-tuple-element.36.in_ref, f32[2,8,2560]{2,1,0:T(8,128)} %pad_maximum_fusion.1.angle_ref), custom_call_target="tpu_custom_call" | custom-call | flops 40000000000 | bytes 10000000 | tf_op jit(solution)/shard_map/attention/pallas_call | solution.py:580
  86.9 0.0 copy-done.1
  86.9 0.0 copy-done.2
  86.9 0.6 add.61
  87.5 168.0 %last.1 = (bf16[160,1024]{1,0:T(8,128)(2,1)}, f32[160,1024]{1,0:T(8,128)}, bf16[98,64,1024]{2,1,0:T(8,128)(2,1)}) custom-call(bf16[16,160,256]{2,1,0:T(8,128)(2,1)} %attention.1.stage, bf16[160,1024]{1,0:T(8,128)(2,1)} %get-tuple-element.37.mlp_in, bf16[160,1024]{1,0:T(8,128)(2,1)} %get-tuple-element.38.gn_in, ...), custom_call_target="tpu_custom_call" | custom-call | tf_op jit(solution)/shard_map/last/pallas_call | solution.py:759
  255.4 17.6 %widen.1 = (f32[1024,1536]{1,0:T(8,128)}, f32[1024,512]{1,0:T(8,128)}, f32[1024,2048]{1,0:T(8,128)}, f32[2,1024,1024]{2,1,0:T(8,128)}, f32[16,1024]{1,0:T(8,128)...) custom-call(bf16[98,64,1024]{2,1,0:T(8,128)(2,1)} %get-tuple-element.46.up_a.up_b.down_a.down_b.first_ref.second_ref.vec_ref, ...), custom_call_target="tpu_custom_call" | custom-call | tf_op jit(solution)/shard_map/widen/pallas_call | solution.py:810
  273.1 0.8 slice.17
  273.8 0.7 dynamic_slice.32
  274.5 1.0 fusion.12
  275.5 0.0 copy-start
  275.5 0.6 constant_dynamic-slice_fusion
  276.1 0.6 constant_dynamic-slice_fusion.1
  276.7 0.8 slice_bitcast_fusion
  277.4 0.6 copy.27
  278.1 0.6 copy.29
  278.6 0.0 copy-done
  (8 shorter events, 0.1 us)
Async XLA Ops:
  10.8 41.4 %copy-start.3 = (s32[16,2]{0,1:T(2,128)S(1)}, s32[16,2]{0,1:T(2,128)}, u32[]{:S(2)}) copy-start(s32[16,2]{0,1:T(2,128)} %param.14) | copy-start | bytes 388
  52.2 1.7 copy-start.4
  53.9 32.9 %copy-start.1 = (f32[1024]{0:T(1024)S(1)}, f32[1024]{0:T(1024)}, u32[]{:S(2)}) copy-start(f32[1024]{0:T(1024)} %param.20) | copy-start | bytes 12292
  53.9 32.9 %copy-start.2 = (f32[1024]{0:T(1024)S(1)}, f32[1024]{0:T(1024)}, u32[]{:S(2)}) copy-start(f32[1024]{0:T(1024)} %param.24) | copy-start | bytes 12292
  275.5 3.1 %copy-start = (f32[1,512]{1,0:T(1,128)}, f32[1,512]{1,0:T(1,128)S(1)}, u32[]{:S(2)}) copy-start(f32[1,512]{1,0:T(1,128)S(1)} %constant_dynamic-slice_fusion.2) | copy-start | bytes 6148
